TPU v7x, 32 devices: a whole 2x2x4 slice. The times are simulated.
32 devices in a mesh: seq: 4 (over y, x), blk: 8 (over z, core).
Axes of the slice: x: 2, y: 2, z: 4, core: 2. Of those that a mesh axis runs over, the one named last changes fastest.
Arguments:
- queries: bfloat16 [4, 2048, 2048], P('seq', 'blk'), may hold values from -150 to 150
- keys: bfloat16 [4, 256, 2048], P('seq', 'blk'), may hold values from -6 to 6
- values: bfloat16 [4, 256, 2048], P('seq', 'blk'), may hold values from -6 to 6
- image_index: int32 [4, 2048], P('seq', 'blk'), may hold values from 0 to 3, as said below
- head_gate: float32 [16], replicated, may hold values from 0.3 to 1.5
- out_weight: bfloat16 [2048, 4096], P(None, 'blk'), may hold values from -0.125 to 0.125
Outputs:
- layer_out: bfloat16 [4, 2048, 4096], P('seq', 'blk')
Inputs may be any that keep to these rules, and one draw needn't show every extreme that they name: Along each sequence image_index never falls; each image's run of text tokens is at least 256 long, so one device's tokens meet at most two images.
All inputs are finite; a program needn't handle non-finite values.
Results may differ from a plain program's by a relative error of at most 0.008.
Values may be sent and summed in bfloat16 or wider, within the bound.
No kernel may reach another device: no remote copies, remote signals or barrier semaphores. Data moves between devices by JAX's collectives and lax.ppermute only.
A program may use at most 128 MiB of HBM per device.

v0:
```python
import functools

import jax
import jax.numpy as jnp
from jax import lax
from jax.experimental import pallas as pl
from jax.experimental.pallas import tpu as pltpu
from jax.sharding import PartitionSpec as P


IMAGES = 4


def attend_kernel(heads, latents, packed, gate_ref, images_ref, latent_image_ref, q_ref, *refs):
    blocks, (out_ref, key_all, value_all) = refs[:-3], refs[-3:]
    at = 0
    for i, together in enumerate(packed):
        rows = slice(i * latents, (i + 1) * latents)
        if together:
            key_all[rows, :] = blocks[at][:latents, :]
            value_all[rows, :] = blocks[at][latents:, :]
            at += 1
        else:
            key_all[rows, :] = blocks[at][...]
            value_all[rows, :] = blocks[at + 1][...]
            at += 2
    size = q_ref.shape[1] // heads
    allowed = latent_image_ref[...] <= images_ref[...]
    for h in range(heads):
        lanes = slice(h * size, (h + 1) * size)
        scores = lax.dot_general(
            q_ref[:, lanes], key_all[:, lanes], (((1,), (1,)), ((), ())), preferred_element_type=jnp.float32
        ) * size ** (-0.5)
        scores = jnp.where(allowed, scores, -1e30)
        probs = jnp.where(allowed, jnp.exp(scores - jnp.max(scores, axis=1, keepdims=True)), 0.0)
        denom = jnp.sum(probs, axis=1, keepdims=True)
        weighted = jnp.dot(probs.astype(jnp.bfloat16), value_all[:, lanes], preferred_element_type=jnp.float32)
        out_ref[:, lanes] = (weighted / denom * gate_ref[:, h : h + 1]).astype(jnp.bfloat16)


def project_kernel(hidden_ref, *refs):
    units, (own_ref, other_ref) = refs[:-2], refs[-2:]
    total, at = None, 0
    for unit in units:
        rows = unit.shape[0]
        part = jnp.dot(hidden_ref[:, at : at + rows], unit[...], preferred_element_type=jnp.float32)
        total = part if total is None else total + part
        at += rows
    tokens = own_ref.shape[0]
    own_ref[...] = total[:tokens].astype(jnp.bfloat16)
    other_ref[...] = total[tokens:].astype(jnp.bfloat16)


def project(hidden, units):
    tokens, cols = hidden.shape[0] // 2, units[0].shape[1]
    shape = jax.ShapeDtypeStruct((tokens, cols), jnp.bfloat16)
    flops = 2 * hidden.shape[0] * hidden.shape[1] * cols
    return pl.pallas_call(
        project_kernel,
        out_shape=(shape, shape),
        cost_estimate=pl.CostEstimate(flops=flops, transcendentals=0, bytes_accessed=hidden.size * 2),
        name="project",
    )(hidden, *units)


def place_kernel(count, where_ref, *refs):
    mine, theirs, out_ref = refs[:count], refs[count : 2 * count], refs[-1]
    cols = mine[0].shape[1]
    step = pl.program_id(0)
    core = where_ref[0]
    for i in range(count):

        @pl.when((step == i) & (core == 0))
        def _():
            out_ref[:, :cols] = mine[i][...]
            out_ref[:, cols:] = theirs[i][...]

        @pl.when((step == i) & (core == 1))
        def _():
            out_ref[:, :cols] = theirs[i][...]
            out_ref[:, cols:] = mine[i][...]


def place(core, at, mine, theirs, chips, out=None):
    count = len(mine)
    tokens, cols = mine[0].shape
    whole = pl.BlockSpec((tokens, cols), lambda i, where: (0, 0))
    before = () if out is None else (out,)
    return pl.pallas_call(
        functools.partial(place_kernel, count),
        grid_spec=pltpu.PrefetchScalarGridSpec(
            num_scalar_prefetch=1,
            grid=(count,),
            in_specs=[whole] * (2 * count) + [pl.BlockSpec(memory_space=pl.ANY)] * len(before),
            out_specs=pl.BlockSpec((tokens, 2 * cols), lambda i, where: (0, where[1 + i])),
        ),
        out_shape=jax.ShapeDtypeStruct((tokens, 2 * cols * chips), jnp.bfloat16),
        input_output_aliases={1 + 2 * count: 0} if before else {},
        name="place",
    )(jnp.stack([core, *at]).astype(jnp.int32), *mine, *theirs, *before)


def steps(chips):
    far = chips // 2
    order = [("kv_up", 1), ("kv_down", 1), ("a_up", 1), ("b_down", 1), ("kv_swap", 0)]
    for k in range(2, far + 1):
        order += [("kv_up", k), ("kv_down", k), ("a_down", k - 1), ("b_up", k - 1)]
        order += [("kv_swap_up", k - 1), ("kv_swap_down", k - 1), ("x_up", k - 1), ("y_down", k - 1)]
        order += [("a_up", k), ("b_down", k)]
        if k > 2:
            order += [("x_down", k - 2), ("y_up", k - 2)]
    order += [("kv_swap_up", far), ("kv_swap_down", far), ("attend", 0), ("hidden_swap", 0)]
    if far > 1:
        order += [("x_down", far - 1), ("y_up", far - 1)]
    order += [("project", 0), ("x_up", far), ("y_down", far)]
    for k in range(1, far):
        order += [("project_up", k), ("project_down", k)]
    return order + [("place", 0), ("project", far), ("place", 1)]


def per_device(queries, keys, values, image_index, head_gate, out_weight):
    blocks, seqs = lax.axis_size("blk"), lax.axis_size("seq")
    chips = blocks // 2
    far = chips // 2
    me, seq = lax.axis_index("blk"), lax.axis_index("seq")
    chip, core = me // 2, me % 2
    parity = (seq ^ (seq >> 1)) & 1
    heads = head_gate.shape[0]
    tokens, width = queries.shape[1:]
    latents = keys.shape[1]

    half = out_weight.shape[0] // 2
    quarter = half // 2
    cols = out_weight.shape[1]
    kv = jnp.concatenate([keys[0], values[0]], axis=0)
    a = lax.dynamic_slice(out_weight, (parity * half, 0), (quarter, cols))
    b = lax.dynamic_slice(out_weight, (parity * half + quarter, 0), (quarter, cols))

    moved = {("kv_up", 0): kv, ("kv_down", 0): kv}
    for name in ("a_up", "a_down"):
        moved[name, 0] = a
    for name in ("b_up", "b_down"):
        moved[name, 0] = b

    def shift(x, by):
        return lax.ppermute(x, "blk", [(i, (i + 2 * by) % blocks) for i in range(blocks)])

    def swap(x):
        return lax.ppermute(x, "blk", [(i, i ^ 1) for i in range(blocks)])

    def side(x, bit):
        return lax.ppermute(x, "seq", [(i, i ^ bit) for i in range(seqs)])

    def attend():
        packed, arrays, first_rows = [], [], []
        for k in range(far + 1):
            for name, d in (("up", -k), ("down", k)) if 0 < k < far else (("", k),):
                for other in range(2):
                    if k == 0:
                        found = [moved["kv_swap", 0] if other else kv]
                    elif k < far:
                        found = [moved[f"kv_swap_{name}" if other else f"kv_{name}", k]]
                    else:
                        found = [moved[f"kv_swap_{n}" if other else f"kv_{n}", k] for n in ("up", "down")]
                    packed.append(len(found) == 1)
                    arrays += found
                    first_rows.append((lax.rem(chip + d + chips, chips) * 2 + (core ^ other)) * latents)
        latent = (jnp.stack(first_rows)[:, None] + lax.iota(jnp.int32, latents)[None, :]).reshape(1, -1)
        latent_image = latent // (latents * blocks // IMAGES)
        return pl.pallas_call(
            functools.partial(attend_kernel, heads, latents, tuple(packed)),
            out_shape=jax.ShapeDtypeStruct((tokens, width), jnp.bfloat16),
            scratch_shapes=[pltpu.VMEM((latents * blocks, width), jnp.bfloat16)] * 2,
            name="attend",
        )(jnp.tanh(head_gate)[None], image_index[0][:, None], latent_image, queries[0], *arrays)

    def units(k, name):
        first = moved["a_up" if name != "down" else "a_down", k]
        second = moved["b_down" if name != "up" else "b_up", k]
        return [first, second, moved["x_down" if name == "down" else "x_up", k], moved["y_up" if name == "up" else "y_down", k]]

    mine, theirs, at = [], [], []
    out = None
    hidden = both = rolled = None
    for name, k in steps(chips):
        if name in ("kv_up", "kv_down") and k == far:
            before = moved[name, k - 1]
            moved[name, k] = shift(before[:latents] if name == "kv_up" else before[latents:], 1 if name == "kv_up" else -1)
        elif name in ("kv_up", "a_up", "b_up"):
            moved[name, k] = shift(moved[name, k - 1], 1)
        elif name in ("kv_down", "a_down", "b_down"):
            moved[name, k] = shift(moved[name, k - 1], -1)
        elif name == "kv_swap":
            moved[name, k] = swap(kv)
        elif name in ("kv_swap_up", "kv_swap_down"):
            moved[name, k] = swap(moved[name.replace("swap_", ""), k])
        elif name in ("x_up", "x_down"):
            moved[name, k] = side(moved[name.replace("x", "a"), k], 1)
        elif name in ("y_up", "y_down"):
            moved[name, k] = side(moved[name.replace("y", "b"), k], 2)
        elif name == "attend":
            hidden = attend()
        elif name == "hidden_swap":
            both = jnp.concatenate([hidden, swap(hidden)], axis=0)
            rolled = jnp.where(parity == 0, both, jnp.concatenate([both[:, half:], both[:, :half]], axis=1))
        elif name == "place":
            out = place(core, at, mine, theirs, chips, out)
            mine, theirs, at = [], [], []
        else:
            which = name[len("project_") :]
            own, other = project(both, [out_weight]) if k == 0 else project(rolled, units(k, which))
            mine.append(own)
            theirs.append(swap(other))
            at.append(lax.rem(chip + chips + (-k if which == "up" else k), chips))
    return out[None]


def solution(mesh):
    placed = (
        P("seq", "blk", None),
        P("seq", "blk", None),
        P("seq", "blk", None),
        P("seq", "blk"),
        P(),
        P(None, "blk"),
    )

    return jax.shard_map(per_device, mesh=mesh, in_specs=placed, out_specs=P("seq", "blk", None), check_vma=False)
```

profile of v0, /device:TPU:0, one launch (start us, length us, event | category | flops | bytes accessed | tf_op | source)
XLA Modules:
  0.0 130.7 jit_solution(11436149928574831983)
XLA Ops:
  1.0 3.1 %collective-permute-start.1 = (bf16[64,2048]{1,0:T(8,128)(2,1)S(1)}, bf16[64,2048]{1,0:T(8,128)(2,1)S(1)}, u32[]{:S(2)}, u32[]{:S(2)}) collective-permute-start(bf16[64,2048]{1,0:T(8,128)(2,1)S(1)} %pad_maximum_fusion.1.refs_0_), channel_id=1, source_target_pairs={{0,2},{1,3},{2,4},{3,5},{4,6},{5,7},{6,0},{7,1},{8,10},{9,11},{10,... | collective-permute-start | bytes 786440 | tf_op jit(solution)/shard_map/ppermute | solution.py:146
  4.1 2.1 %collective-permute-start.3 = (bf16[64,2048]{1,0:T(8,128)(2,1)S(1)}, bf16[64,2048]{1,0:T(8,128)(2,1)S(1)}, u32[]{:S(2)}, u32[]{:S(2)}) collective-permute-start(bf16[64,2048]{1,0:T(8,128)(2,1)S(1)} %pad_maximum_fusion.1.refs_0_), channel_id=1, source_target_pairs={{0,6},{1,7},{2,0},{3,1},{4,2},{5,3},{6,4},{7,5},{8,14},{9,15},{10,... | collective-permute-start | bytes 786440 | tf_op jit(solution)/shard_map/ppermute | solution.py:146
  6.4 1.5 %copy.8.images_ref = s32[256,1]{1,0:T(8,128)} copy(s32[256,1]{0,1:T(1,128)} %bitcast.23) | data formatting | bytes 2048 | tf_op jit(solution)/shard_map/broadcast_in_dim;squeeze | solution.py:175
  8.5 4.8 %collective-permute-done.1.refs_2_ = bf16[64,2048]{1,0:T(8,128)(2,1)S(1)} collective-permute-done((bf16[64,2048]{1,0:T(8,128)(2,1)S(1)}, bf16[64,2048]{1,0:T(8,128)(2,1)S(1)}, u32[]{:S(2)}, u32[]{:S(2)}) %collective-permute-start.1) | collective-permute-done | bytes 262176 | tf_op jit(solution)/shard_map/ppermute | solution.py:146
  13.4 4.3 %collective-permute-done.3.refs_4_ = bf16[64,2048]{1,0:T(8,128)(2,1)S(1)} collective-permute-done((bf16[64,2048]{1,0:T(8,128)(2,1)S(1)}, bf16[64,2048]{1,0:T(8,128)(2,1)S(1)}, u32[]{:S(2)}, u32[]{:S(2)}) %collective-permute-start.3) | collective-permute-done | bytes 262176 | tf_op jit(solution)/shard_map/ppermute | solution.py:146
  17.7 3.1 %collective-permute-start.6 = (bf16[32,2048]{1,0:T(8,128)(2,1)S(1)}, bf16[32,2048]{1,0:T(8,128)(2,1)S(1)}, u32[]{:S(2)}, u32[]{:S(2)}) collective-permute-start(bf16[32,2048]{1,0:T(8,128)(2,1)S(1)} %slice.17), channel_id=1, source_target_pairs={{0,6},{1,7},{2,0},{3,1},{4,2},{5,3},{6,4},{7,5},{8,14},{9,15},{10,... | collective-permute-start | bytes 393224 | tf_op jit(solution)/shard_map/ppermute | solution.py:146
  22.9 1.5 %collective-permute-done.6.refs_7_ = bf16[32,2048]{1,0:T(8,128)(2,1)S(1)} collective-permute-done((bf16[32,2048]{1,0:T(8,128)(2,1)S(1)}, bf16[32,2048]{1,0:T(8,128)(2,1)S(1)}, u32[]{:S(2)}, u32[]{:S(2)}) %collective-permute-start.6) | collective-permute-done | bytes 131104 | tf_op jit(solution)/shard_map/ppermute | solution.py:146
  24.5 1.3 %constant_dynamic-slice_fusion = (bf16[512,512]{1,0:T(8,128)(2,1)S(1)}, bf16[512,512]{1,0:T(8,128)(2,1)S(1)}) fusion(bf16[2048,512]{1,0:T(8,128)(2,1)} %refs_0_.1, s32[]{:T(128)S(6)} %select_n.36, s32[]{:T(128)S(6)} %select_n.35), kind=kLoop, calls=%fused_computation.17 | loop fusion | bytes 2097160 | tf_op jit(solution)/shard_map/dynamic_slice | solution.py:137
  25.8 3.2 %collective-permute-start.12 = (bf16[512,512]{1,0:T(8,128)(2,1)S(1)}, bf16[512,512]{1,0:T(8,128)(2,1)S(1)}, u32[]{:S(2)}, u32[]{:S(2)}) collective-permute-start(bf16[512,512]{1,0:T(8,128)(2,1)S(1)} %get-tuple-element.23), channel_id=1, source_target_pairs={{0,6},{1,7},{2,0},{3,1},{4,2},{5,3},{6,4},{7,5},{8,14},{9,15},{10,... | collective-permute-start | bytes 1572872 | tf_op jit(solution)/shard_map/ppermute | solution.py:146
  30.4 5.5 %attend.1 = bf16[256,2048]{1,0:T(8,128)(2,1)} custom-call(f32[1,16]{1,0:T(1,128)} %tanh_bitcast_fusion.gate_ref, s32[256,1]{1,0:T(8,128)} %copy.8.images_ref, s32[1,256]{1,0:T(1,128)} %and_select_fusion.latent_image_ref, bf16[256,2048]{1,0:T(8,128)(2,1)} %bitcast.20, bf16[64,2048]{1,0:T(8,128)(2,1)} %copy-done.1, bf16[64,2048]{1,0:T(8,128)(2,1)} %copy-done.10, ...), custom_call_target="tpu_custom_call" | custom-call | tf_op jit(solution)/shard_map/attend/pallas_call | solution.py:170
  36.0 3.8 %collective-permute-start.20 = (bf16[512,512]{1,0:T(8,128)(2,1)S(1)}, bf16[512,512]{1,0:T(8,128)(2,1)}, u32[]{:S(2)}, u32[]{:S(2)}) collective-permute-start(bf16[512,512]{1,0:T(8,128)(2,1)S(1)} %get-tuple-element.24), channel_id=1, source_target_pairs={{0,6},{1,7},{2,0},{3,1},{4,2},{5,3},{6,4},{7,5},{8,14},{9,15},{10,... | collective-permute-start | bytes 1572872 | tf_op jit(solution)/shard_map/ppermute | solution.py:146
  39.9 1.5 %collective-permute-done.12.refs_1_ = bf16[512,512]{1,0:T(8,128)(2,1)S(1)} collective-permute-done((bf16[512,512]{1,0:T(8,128)(2,1)S(1)}, bf16[512,512]{1,0:T(8,128)(2,1)S(1)}, u32[]{:S(2)}, u32[]{:S(2)}) %collective-permute-start.12) | collective-permute-done | bytes 524320 | tf_op jit(solution)/shard_map/ppermute | solution.py:146
  41.3 1.5 %collective-permute-start.22 = (bf16[512,512]{1,0:T(8,128)(2,1)S(1)}, bf16[512,512]{1,0:T(8,128)(2,1)}, u32[]{:S(2)}, u32[]{:S(2)}) collective-permute-start(bf16[512,512]{1,0:T(8,128)(2,1)S(1)} %collective-permute-done.12.refs_1_), channel_id=1, source_target_pairs={{0,16},{8,24},{16,0},{24,8},{1,17},{9,25},{17,1},{25,9},{2,18},{10... | collective-permute-start | bytes 1572872 | tf_op jit(solution)/shard_map/ppermute | solution.py:152
  42.9 10.3 %collective-permute-done.10.refs_0_ = bf16[512,512]{1,0:T(8,128)(2,1)} collective-permute-done((bf16[512,512]{1,0:T(8,128)(2,1)S(1)}, bf16[512,512]{1,0:T(8,128)(2,1)}, u32[]{:S(2)}, u32[]{:S(2)}) %collective-permute-start.10) | collective-permute-done | bytes 524320 | tf_op jit(solution)/shard_map/ppermute | solution.py:146
  53.1 2.0 %collective-permute-start.11 = (bf16[512,512]{1,0:T(8,128)(2,1)}, bf16[512,512]{1,0:T(8,128)(2,1)S(1)}, u32[]{:S(2)}, u32[]{:S(2)}) collective-permute-start(bf16[512,512]{1,0:T(8,128)(2,1)} %collective-permute-done.10.refs_0_), channel_id=1, source_target_pairs={{0,2},{1,3},{2,4},{3,5},{4,6},{5,7},{6,0},{7,1},{8,10},{9,11},{10,... | collective-permute-start | bytes 1572872 | tf_op jit(solution)/shard_map/ppermute | solution.py:146
  55.2 8.7 %collective-permute-done.20.refs_0_ = bf16[512,512]{1,0:T(8,128)(2,1)} collective-permute-done((bf16[512,512]{1,0:T(8,128)(2,1)S(1)}, bf16[512,512]{1,0:T(8,128)(2,1)}, u32[]{:S(2)}, u32[]{:S(2)}) %collective-permute-start.20) | collective-permute-done | bytes 524320 | tf_op jit(solution)/shard_map/ppermute | solution.py:146
  63.9 4.4 %collective-permute-start.13 = (bf16[512,512]{1,0:T(8,128)(2,1)S(1)}, bf16[512,512]{1,0:T(8,128)(2,1)S(1)}, u32[]{:S(2)}, u32[]{:S(2)}) collective-permute-start(bf16[512,512]{1,0:T(8,128)(2,1)S(1)} %collective-permute-done.12.refs_1_), channel_id=1, source_target_pairs={{0,6},{1,7},{2,0},{3,1},{4,2},{5,3},{6,4},{7,5},{8,14},{9,15},{10,... | collective-permute-start | bytes 1572872 | tf_op jit(solution)/shard_map/ppermute | solution.py:146
  68.2 7.4 %collective-permute-done.17.refs_1_ = bf16[512,512]{1,0:T(8,128)(2,1)S(1)} collective-permute-done((bf16[512,512]{1,0:T(8,128)(2,1)S(1)}, bf16[512,512]{1,0:T(8,128)(2,1)S(1)}, u32[]{:S(2)}, u32[]{:S(2)}) %collective-permute-start.17) | collective-permute-done | bytes 524320 | tf_op jit(solution)/shard_map/ppermute | solution.py:146
  76.4 1.5 %collective-permute-start.21 = (bf16[512,512]{1,0:T(8,128)(2,1)}, bf16[512,512]{1,0:T(8,128)(2,1)}, u32[]{:S(2)}, u32[]{:S(2)}) collective-permute-start(bf16[512,512]{1,0:T(8,128)(2,1)} %collective-permute-done.20.refs_0_), channel_id=1, source_target_pairs={{0,8},{8,0},{16,24},{24,16},{1,9},{9,1},{17,25},{25,17},{2,10},{10... | collective-permute-start | bytes 1572872 | tf_op jit(solution)/shard_map/ppermute | solution.py:152
  78.4 1.5 %collective-permute-start.19 = (bf16[512,512]{1,0:T(8,128)(2,1)}, bf16[512,512]{1,0:T(8,128)(2,1)}, u32[]{:S(2)}, u32[]{:S(2)}) collective-permute-start(bf16[512,512]{1,0:T(8,128)(2,1)} %copy-done.7), channel_id=1, source_target_pairs={{0,16},{8,24},{16,0},{24,8},{1,17},{9,25},{17,1},{25,9},{2,18},{10... | collective-permute-start | bytes 1572872 | tf_op jit(solution)/shard_map/ppermute | solution.py:152
  80.0 1.4 %fusion = (bf16[512,1024]{1,0:T(8,128)(2,1)S(1)}, bf16[512,1024]{1,0:T(8,128)(2,1)S(1)}) fusion(bf16[256,2048]{1,0:T(8,128)(2,1)} %attend.1, bf16[256,2048]{1,0:T(8,128)(2,1)S(1)} %collective-permute-done.9), kind=kLoop, calls=%fused_computation.6 | loop fusion | flops 4194304 | bytes 4194304 | tf_op jit(solution)/shard_map/concatenate | solution.py:204
  81.3 5.4 %collective-permute-done.11.refs_0_ = bf16[512,512]{1,0:T(8,128)(2,1)S(1)} collective-permute-done((bf16[512,512]{1,0:T(8,128)(2,1)}, bf16[512,512]{1,0:T(8,128)(2,1)S(1)}, u32[]{:S(2)}, u32[]{:S(2)}) %collective-permute-start.11) | collective-permute-done | bytes 524320 | tf_op jit(solution)/shard_map/ppermute | solution.py:146
  86.8 1.5 %collective-permute-start.14 = (bf16[512,512]{1,0:T(8,128)(2,1)S(1)}, bf16[512,512]{1,0:T(8,128)(2,1)S(1)}, u32[]{:S(2)}, u32[]{:S(2)}) collective-permute-start(bf16[512,512]{1,0:T(8,128)(2,1)S(1)} %collective-permute-done.11.refs_0_), channel_id=1, source_target_pairs={{0,8},{8,0},{16,24},{24,16},{1,9},{9,1},{17,25},{25,17},{2,10},{10... | collective-permute-start | bytes 1572872 | tf_op jit(solution)/shard_map/ppermute | solution.py:152
  88.3 9.5 %collective-permute-done.13.refs_1_ = bf16[512,512]{1,0:T(8,128)(2,1)S(1)} collective-permute-done((bf16[512,512]{1,0:T(8,128)(2,1)S(1)}, bf16[512,512]{1,0:T(8,128)(2,1)S(1)}, u32[]{:S(2)}, u32[]{:S(2)}) %collective-permute-start.13) | collective-permute-done | bytes 524320 | tf_op jit(solution)/shard_map/ppermute | solution.py:146
  97.8 1.5 %collective-permute-start.15 = (bf16[512,512]{1,0:T(8,128)(2,1)S(1)}, bf16[512,512]{1,0:T(8,128)(2,1)S(1)}, u32[]{:S(2)}, u32[]{:S(2)}) collective-permute-start(bf16[512,512]{1,0:T(8,128)(2,1)S(1)} %collective-permute-done.13.refs_1_), channel_id=1, source_target_pairs={{0,16},{8,24},{16,0},{24,8},{1,17},{9,25},{17,1},{25,9},{2,18},{10... | collective-permute-start | bytes 1572872 | tf_op jit(solution)/shard_map/ppermute | solution.py:152
  99.3 3.1 %pad_maximum_fusion = (bf16[512,2048]{1,0:T(8,128)(2,1)}, bf16[512,2048]{1,0:T(8,128)(2,1)}) fusion(bf16[256,2048]{1,0:T(8,128)(2,1)S(1)} %collective-permute-done.9, bf16[256,2048]{1,0:T(8,128)(2,1)S(1)} %copy-done, bf16[512,1024]{1,0:T(8,128)(2,1)S(1)} %get-tuple-element.26, bf16[512,1024]{1,0:T(8,128)(2,1)S(1)} %get-tuple-element.25, pred[]{:T(512)S(6)} %eq.5), kind=kLoop, calls=%fused_computation.2 | loop fusion | flops 9437184 | bytes 8388609 | tf_op jit(solution)/shard_map/concatenate | solution.py:204
  102.4 4.2 %project.7 = (bf16[256,512]{1,0:T(8,128)(2,1)}, bf16[256,512]{1,0:T(8,128)(2,1)}) custom-call(bf16[512,2048]{1,0:T(8,128)(2,1)} %get-tuple-element.22.hidden_ref, bf16[512,512]{1,0:T(8,128)(2,1)} %collective-permute-done.20.refs_0_, bf16[512,512]{1,0:T(8,128)(2,1)} %copy-done.4, bf16[512,512]{1,0:T(8,128)(2,1)} %collective-permute-done.21.refs_2_, ...), custom_call_target="tpu_custom_call" | custom-call | flops 1073741824 | bytes 2097152 | tf_op jit(solution)/shard_map/project/pallas_call | solution.py:58
  106.6 4.1 %project.6 = (bf16[256,512]{1,0:T(8,128)(2,1)}, bf16[256,512]{1,0:T(8,128)(2,1)}) custom-call(bf16[512,2048]{1,0:T(8,128)(2,1)} %get-tuple-element.22.hidden_ref, bf16[512,512]{1,0:T(8,128)(2,1)} %collective-permute-done.10.refs_0_, bf16[512,512]{1,0:T(8,128)(2,1)} %copy-done.7, bf16[512,512]{1,0:T(8,128)(2,1)} %collective-permute-done.18.refs_2_, ...), custom_call_target="tpu_custom_call" | custom-call | flops 1073741824 | bytes 2097152 | tf_op jit(solution)/shard_map/project/pallas_call | solution.py:58
  111.2 4.2 %project.5 = (bf16[256,512]{1,0:T(8,128)(2,1)}, bf16[256,512]{1,0:T(8,128)(2,1)}) custom-call(bf16[512,2048]{1,0:T(8,128)(2,1)} %get-tuple-element.21.hidden_ref, bf16[2048,512]{1,0:T(8,128)(2,1)} %refs_0_.1), custom_call_target="tpu_custom_call" | custom-call | flops 1073741824 | bytes 2097152 | tf_op jit(solution)/shard_map/project/pallas_call | solution.py:58
  117.0 4.1 %project.4 = (bf16[256,512]{1,0:T(8,128)(2,1)}, bf16[256,512]{1,0:T(8,128)(2,1)}) custom-call(bf16[512,2048]{1,0:T(8,128)(2,1)} %get-tuple-element.22.hidden_ref, bf16[512,512]{1,0:T(8,128)(2,1)} %copy-done.5, bf16[512,512]{1,0:T(8,128)(2,1)} %copy-done.6, bf16[512,512]{1,0:T(8,128)(2,1)} %copy-done.8, bf16[512,512]{1,0:T(8,128)(2,1)} %copy-done.9), custom_call_target="tpu_custom_call" | custom-call | flops 1073741824 | bytes 2097152 | tf_op jit(solution)/shard_map/project/pallas_call | solution.py:58
  123.7 3.7 %place.2.refs_2_ = bf16[256,4096]{1,0:T(8,128)(2,1)} custom-call(s32[4]{0:T(128)} %pad_add_fusion.1.where_ref, bf16[256,512]{1,0:T(8,128)(2,1)} %get-tuple-element.15.refs_0_, bf16[256,512]{1,0:T(8,128)(2,1)} %get-tuple-element.16.refs_1_, bf16[256,512]{1,0:T(8,128)(2,1)} %get-tuple-element.17.refs_2_, bf16[256,512]{1,0:T(8,128)(2,1)} %copy-done.16, ...), custom_call_target="tpu_custom_call" | custom-call | tf_op jit(solution)/shard_map/place/pallas_call | solution.py:89
  128.2 2.5 %place.3 = bf16[256,4096]{1,0:T(8,128)(2,1)} custom-call(s32[2]{0:T(128)} %pad_add_fusion.where_ref, bf16[256,512]{1,0:T(8,128)(2,1)} %get-tuple-element.13.refs_0_, bf16[256,512]{1,0:T(8,128)(2,1)} %copy-done.13, bf16[256,4096]{1,0:T(8,128)(2,1)} %place.2.refs_2_), custom_call_target="tpu_custom_call", output_to_operand_aliasing={{}: (3, {})} | custom-call | tf_op jit(solution)/shard_map/place/pallas_call | solution.py:89
  (83 shorter events, 12.3 us)
Async XLA Ops:
  1.0 28.7 %copy-start.1 = (bf16[64,2048]{1,0:T(8,128)(2,1)}, bf16[64,2048]{1,0:T(8,128)(2,1)S(1)}, u32[]{:S(2)}) copy-start(bf16[64,2048]{1,0:T(8,128)(2,1)S(1)} %pad_maximum_fusion.1.refs_0_) | copy-start | bytes 786436
  1.0 12.3 %collective-permute-start.1 = (bf16[64,2048]{1,0:T(8,128)(2,1)S(1)}, bf16[64,2048]{1,0:T(8,128)(2,1)S(1)}, u32[]{:S(2)}, u32[]{:S(2)}) collective-permute-start(bf16[64,2048]{1,0:T(8,128)(2,1)S(1)} %pad_maximum_fusion.1.refs_0_), channel_id=1, source_target_pairs={{0,2},{1,3},{2,4},{3,5},{4,6},{5,7},{6,0},{7,1},{8,10},{9,11},{10,... | collective-permute-start | bytes 786440 | tf_op jit(solution)/shard_map/ppermute | solution.py:146
  4.1 13.6 %collective-permute-start.3 = (bf16[64,2048]{1,0:T(8,128)(2,1)S(1)}, bf16[64,2048]{1,0:T(8,128)(2,1)S(1)}, u32[]{:S(2)}, u32[]{:S(2)}) collective-permute-start(bf16[64,2048]{1,0:T(8,128)(2,1)S(1)} %pad_maximum_fusion.1.refs_0_), channel_id=1, source_target_pairs={{0,6},{1,7},{2,0},{3,1},{4,2},{5,3},{6,4},{7,5},{8,14},{9,15},{10,... | collective-permute-start | bytes 786440 | tf_op jit(solution)/shard_map/ppermute | solution.py:146
  6.2 19.6 %collective-permute-start = (bf16[64,2048]{1,0:T(8,128)(2,1)S(1)}, bf16[64,2048]{1,0:T(8,128)(2,1)S(1)}, u32[]{:S(2)}, u32[]{:S(2)}) collective-permute-start(bf16[64,2048]{1,0:T(8,128)(2,1)S(1)} %pad_maximum_fusion.1.refs_0_), channel_id=1, source_target_pairs={{0,1},{1,0},{2,3},{3,2},{4,5},{5,4},{6,7},{7,6},{8,9},{9,8},{10,11... | collective-permute-start | bytes 786440 | tf_op jit(solution)/shard_map/ppermute | solution.py:149
  13.3 16.4 %copy-start.2 = (bf16[64,2048]{1,0:T(8,128)(2,1)}, bf16[64,2048]{1,0:T(8,128)(2,1)S(1)}, u32[]{:S(2)}) copy-start(bf16[64,2048]{1,0:T(8,128)(2,1)S(1)} %collective-permute-done.1.refs_2_) | copy-start | bytes 786436
  13.3 9.6 %collective-permute-start.5 = (bf16[32,2048]{1,0:T(8,128)(2,1)S(1)}, bf16[32,2048]{1,0:T(8,128)(2,1)S(1)}, u32[]{:S(2)}, u32[]{:S(2)}) collective-permute-start(bf16[32,2048]{1,0:T(8,128)(2,1)S(1)} %slice.16), channel_id=1, source_target_pairs={{0,2},{1,3},{2,4},{3,5},{4,6},{5,7},{6,0},{7,1},{8,10},{9,11},{10,... | collective-permute-start | bytes 393224 | tf_op jit(solution)/shard_map/ppermute | solution.py:146
  17.7 12.0 %copy-start.3 = (bf16[64,2048]{1,0:T(8,128)(2,1)}, bf16[64,2048]{1,0:T(8,128)(2,1)S(1)}, u32[]{:S(2)}) copy-start(bf16[64,2048]{1,0:T(8,128)(2,1)S(1)} %collective-permute-done.3.refs_4_) | copy-start | bytes 786436
  17.7 6.7 %collective-permute-start.6 = (bf16[32,2048]{1,0:T(8,128)(2,1)S(1)}, bf16[32,2048]{1,0:T(8,128)(2,1)S(1)}, u32[]{:S(2)}, u32[]{:S(2)}) collective-permute-start(bf16[32,2048]{1,0:T(8,128)(2,1)S(1)} %slice.17), channel_id=1, source_target_pairs={{0,6},{1,7},{2,0},{3,1},{4,2},{5,3},{6,4},{7,5},{8,14},{9,15},{10,... | collective-permute-start | bytes 393224 | tf_op jit(solution)/shard_map/ppermute | solution.py:146
  20.8 8.2 %collective-permute-start.2 = (bf16[64,2048]{1,0:T(8,128)(2,1)S(1)}, bf16[64,2048]{1,0:T(8,128)(2,1)S(1)}, u32[]{:S(2)}, u32[]{:S(2)}) collective-permute-start(bf16[64,2048]{1,0:T(8,128)(2,1)S(1)} %collective-permute-done.1.refs_2_), channel_id=1, source_target_pairs={{0,1},{1,0},{2,3},{3,2},{4,5},{5,4},{6,7},{7,6},{8,9},{9,8},{10,11... | collective-permute-start | bytes 786440 | tf_op jit(solution)/shard_map/ppermute | solution.py:149
  20.8 8.2 %collective-permute-start.4 = (bf16[64,2048]{1,0:T(8,128)(2,1)S(1)}, bf16[64,2048]{1,0:T(8,128)(2,1)S(1)}, u32[]{:S(2)}, u32[]{:S(2)}) collective-permute-start(bf16[64,2048]{1,0:T(8,128)(2,1)S(1)} %collective-permute-done.3.refs_4_), channel_id=1, source_target_pairs={{0,1},{1,0},{2,3},{3,2},{4,5},{5,4},{6,7},{7,6},{8,9},{9,8},{10,11... | collective-permute-start | bytes 786440 | tf_op jit(solution)/shard_map/ppermute | solution.py:149
  22.9 6.1 %collective-permute-start.7 = (bf16[32,2048]{1,0:T(8,128)(2,1)S(1)}, bf16[32,2048]{1,0:T(8,128)(2,1)S(1)}, u32[]{:S(2)}, u32[]{:S(2)}) collective-permute-start(bf16[32,2048]{1,0:T(8,128)(2,1)S(1)} %collective-permute-done.5.refs_6_), channel_id=1, source_target_pairs={{0,1},{1,0},{2,3},{3,2},{4,5},{5,4},{6,7},{7,6},{8,9},{9,8},{10,11... | collective-permute-start | bytes 393224 | tf_op jit(solution)/shard_map/ppermute | solution.py:149
  24.5 4.5 %collective-permute-start.8 = (bf16[32,2048]{1,0:T(8,128)(2,1)S(1)}, bf16[32,2048]{1,0:T(8,128)(2,1)S(1)}, u32[]{:S(2)}, u32[]{:S(2)}) collective-permute-start(bf16[32,2048]{1,0:T(8,128)(2,1)S(1)} %collective-permute-done.6.refs_7_), channel_id=1, source_target_pairs={{0,1},{1,0},{2,3},{3,2},{4,5},{5,4},{6,7},{7,6},{8,9},{9,8},{10,11... | collective-permute-start | bytes 393224 | tf_op jit(solution)/shard_map/ppermute | solution.py:149
  25.8 15.5 %collective-permute-start.12 = (bf16[512,512]{1,0:T(8,128)(2,1)S(1)}, bf16[512,512]{1,0:T(8,128)(2,1)S(1)}, u32[]{:S(2)}, u32[]{:S(2)}) collective-permute-start(bf16[512,512]{1,0:T(8,128)(2,1)S(1)} %get-tuple-element.23), channel_id=1, source_target_pairs={{0,6},{1,7},{2,0},{3,1},{4,2},{5,3},{6,4},{7,5},{8,14},{9,15},{10,... | collective-permute-start | bytes 1572872 | tf_op jit(solution)/shard_map/ppermute | solution.py:146
  35.9 42.6 %collective-permute-start.9 = (bf16[256,2048]{1,0:T(8,128)(2,1)}, bf16[256,2048]{1,0:T(8,128)(2,1)S(1)}, u32[]{:S(2)}, u32[]{:S(2)}) collective-permute-start(bf16[256,2048]{1,0:T(8,128)(2,1)} %attend.1), channel_id=1, source_target_pairs={{0,1},{1,0},{2,3},{3,2},{4,5},{5,4},{6,7},{7,6},{8,9},{9,8},{10,11... | collective-permute-start | bytes 3145736 | tf_op jit(solution)/shard_map/ppermute | solution.py:149
  36.0 17.1 %collective-permute-start.10 = (bf16[512,512]{1,0:T(8,128)(2,1)S(1)}, bf16[512,512]{1,0:T(8,128)(2,1)}, u32[]{:S(2)}, u32[]{:S(2)}) collective-permute-start(bf16[512,512]{1,0:T(8,128)(2,1)S(1)} %get-tuple-element.24), channel_id=1, source_target_pairs={{0,2},{1,3},{2,4},{3,5},{4,6},{5,7},{6,0},{7,1},{8,10},{9,11},{10,... | collective-permute-start | bytes 1572872 | tf_op jit(solution)/shard_map/ppermute | solution.py:146
  36.0 27.8 %collective-permute-start.20 = (bf16[512,512]{1,0:T(8,128)(2,1)S(1)}, bf16[512,512]{1,0:T(8,128)(2,1)}, u32[]{:S(2)}, u32[]{:S(2)}) collective-permute-start(bf16[512,512]{1,0:T(8,128)(2,1)S(1)} %get-tuple-element.24), channel_id=1, source_target_pairs={{0,6},{1,7},{2,0},{3,1},{4,2},{5,3},{6,4},{7,5},{8,14},{9,15},{10,... | collective-permute-start | bytes 1572872 | tf_op jit(solution)/shard_map/ppermute | solution.py:146
  39.9 35.7 %collective-permute-start.17 = (bf16[512,512]{1,0:T(8,128)(2,1)S(1)}, bf16[512,512]{1,0:T(8,128)(2,1)S(1)}, u32[]{:S(2)}, u32[]{:S(2)}) collective-permute-start(bf16[512,512]{1,0:T(8,128)(2,1)S(1)} %get-tuple-element.23), channel_id=1, source_target_pairs={{0,2},{1,3},{2,4},{3,5},{4,6},{5,7},{6,0},{7,1},{8,10},{9,11},{10,... | collective-permute-start | bytes 1572872 | tf_op jit(solution)/shard_map/ppermute | solution.py:146
  41.3 40.0 %copy-start.4 = (bf16[512,512]{1,0:T(8,128)(2,1)}, bf16[512,512]{1,0:T(8,128)(2,1)S(1)}, u32[]{:S(2)}) copy-start(bf16[512,512]{1,0:T(8,128)(2,1)S(1)} %collective-permute-done.12.refs_1_) | copy-start | bytes 1572868
  41.3 36.6 %collective-permute-start.22 = (bf16[512,512]{1,0:T(8,128)(2,1)S(1)}, bf16[512,512]{1,0:T(8,128)(2,1)}, u32[]{:S(2)}, u32[]{:S(2)}) collective-permute-start(bf16[512,512]{1,0:T(8,128)(2,1)S(1)} %collective-permute-done.12.refs_1_), channel_id=1, source_target_pairs={{0,16},{8,24},{16,0},{24,8},{1,17},{9,25},{17,1},{25,9},{2,18},{10... | collective-permute-start | bytes 1572872 | tf_op jit(solution)/shard_map/ppermute | solution.py:152
  53.1 33.6 %collective-permute-start.11 = (bf16[512,512]{1,0:T(8,128)(2,1)}, bf16[512,512]{1,0:T(8,128)(2,1)S(1)}, u32[]{:S(2)}, u32[]{:S(2)}) collective-permute-start(bf16[512,512]{1,0:T(8,128)(2,1)} %collective-permute-done.10.refs_0_), channel_id=1, source_target_pairs={{0,2},{1,3},{2,4},{3,5},{4,6},{5,7},{6,0},{7,1},{8,10},{9,11},{10,... | collective-permute-start | bytes 1572872 | tf_op jit(solution)/shard_map/ppermute | solution.py:146
  63.9 33.9 %collective-permute-start.13 = (bf16[512,512]{1,0:T(8,128)(2,1)S(1)}, bf16[512,512]{1,0:T(8,128)(2,1)S(1)}, u32[]{:S(2)}, u32[]{:S(2)}) collective-permute-start(bf16[512,512]{1,0:T(8,128)(2,1)S(1)} %collective-permute-done.12.refs_1_), channel_id=1, source_target_pairs={{0,6},{1,7},{2,0},{3,1},{4,2},{5,3},{6,4},{7,5},{8,14},{9,15},{10,... | collective-permute-start | bytes 1572872 | tf_op jit(solution)/shard_map/ppermute | solution.py:146
  76.4 26.0 %collective-permute-start.21 = (bf16[512,512]{1,0:T(8,128)(2,1)}, bf16[512,512]{1,0:T(8,128)(2,1)}, u32[]{:S(2)}, u32[]{:S(2)}) collective-permute-start(bf16[512,512]{1,0:T(8,128)(2,1)} %collective-permute-done.20.refs_0_), channel_id=1, source_target_pairs={{0,8},{8,0},{16,24},{24,16},{1,9},{9,1},{17,25},{25,17},{2,10},{10... | collective-permute-start | bytes 1572872 | tf_op jit(solution)/shard_map/ppermute | solution.py:152
  77.9 21.4 %copy-start = (bf16[256,2048]{1,0:T(8,128)(2,1)S(1)}, bf16[256,2048]{1,0:T(8,128)(2,1)}, u32[]{:S(2)}) copy-start(bf16[256,2048]{1,0:T(8,128)(2,1)} %attend.1) | copy-start | bytes 3145732
  77.9 28.6 %collective-permute-start.18 = (bf16[512,512]{1,0:T(8,128)(2,1)}, bf16[512,512]{1,0:T(8,128)(2,1)}, u32[]{:S(2)}, u32[]{:S(2)}) collective-permute-start(bf16[512,512]{1,0:T(8,128)(2,1)} %collective-permute-done.10.refs_0_), channel_id=1, source_target_pairs={{0,8},{8,0},{16,24},{24,16},{1,9},{9,1},{17,25},{25,17},{2,10},{10... | collective-permute-start | bytes 1572872 | tf_op jit(solution)/shard_map/ppermute | solution.py:152
  78.4 28.1 %collective-permute-start.19 = (bf16[512,512]{1,0:T(8,128)(2,1)}, bf16[512,512]{1,0:T(8,128)(2,1)}, u32[]{:S(2)}, u32[]{:S(2)}) collective-permute-start(bf16[512,512]{1,0:T(8,128)(2,1)} %copy-done.7), channel_id=1, source_target_pairs={{0,16},{8,24},{16,0},{24,8},{1,17},{9,25},{17,1},{25,9},{2,18},{10... | collective-permute-start | bytes 1572872 | tf_op jit(solution)/shard_map/ppermute | solution.py:152
  86.8 15.6 %copy-start.5 = (bf16[512,512]{1,0:T(8,128)(2,1)}, bf16[512,512]{1,0:T(8,128)(2,1)S(1)}, u32[]{:S(2)}) copy-start(bf16[512,512]{1,0:T(8,128)(2,1)S(1)} %collective-permute-done.11.refs_0_) | copy-start | bytes 1572868
  86.8 28.6 %collective-permute-start.14 = (bf16[512,512]{1,0:T(8,128)(2,1)S(1)}, bf16[512,512]{1,0:T(8,128)(2,1)S(1)}, u32[]{:S(2)}, u32[]{:S(2)}) collective-permute-start(bf16[512,512]{1,0:T(8,128)(2,1)S(1)} %collective-permute-done.11.refs_0_), channel_id=1, source_target_pairs={{0,8},{8,0},{16,24},{24,16},{1,9},{9,1},{17,25},{25,17},{2,10},{10... | collective-permute-start | bytes 1572872 | tf_op jit(solution)/shard_map/ppermute | solution.py:152
  97.8 17.7 %collective-permute-start.15 = (bf16[512,512]{1,0:T(8,128)(2,1)S(1)}, bf16[512,512]{1,0:T(8,128)(2,1)S(1)}, u32[]{:S(2)}, u32[]{:S(2)}) collective-permute-start(bf16[512,512]{1,0:T(8,128)(2,1)S(1)} %collective-permute-done.13.refs_1_), channel_id=1, source_target_pairs={{0,16},{8,24},{16,0},{24,8},{1,17},{9,25},{17,1},{25,9},{2,18},{10... | collective-permute-start | bytes 1572872 | tf_op jit(solution)/shard_map/ppermute | solution.py:152
  106.5 16.3 %collective-permute-start.25 = (bf16[256,512]{1,0:T(8,128)(2,1)}, bf16[256,512]{1,0:T(8,128)(2,1)S(1)}, u32[]{:S(2)}, u32[]{:S(2)}) collective-permute-start(bf16[256,512]{1,0:T(8,128)(2,1)} %get-tuple-element.20), channel_id=1, source_target_pairs={{0,1},{1,0},{2,3},{3,2},{4,5},{5,4},{6,7},{7,6},{8,9},{9,8},{10,11... | collective-permute-start | bytes 786440 | tf_op jit(solution)/shard_map/ppermute | solution.py:149
  110.7 12.1 %collective-permute-start.24 = (bf16[256,512]{1,0:T(8,128)(2,1)}, bf16[256,512]{1,0:T(8,128)(2,1)S(1)}, u32[]{:S(2)}, u32[]{:S(2)}) collective-permute-start(bf16[256,512]{1,0:T(8,128)(2,1)} %get-tuple-element.19), channel_id=1, source_target_pairs={{0,1},{1,0},{2,3},{3,2},{4,5},{5,4},{6,7},{7,6},{8,9},{9,8},{10,11... | collective-permute-start | bytes 786440 | tf_op jit(solution)/shard_map/ppermute | solution.py:149
  115.4 7.5 %collective-permute-start.23 = (bf16[256,512]{1,0:T(8,128)(2,1)}, bf16[256,512]{1,0:T(8,128)(2,1)S(1)}, u32[]{:S(2)}, u32[]{:S(2)}) collective-permute-start(bf16[256,512]{1,0:T(8,128)(2,1)} %get-tuple-element.18), channel_id=1, source_target_pairs={{0,1},{1,0},{2,3},{3,2},{4,5},{5,4},{6,7},{7,6},{8,9},{9,8},{10,11... | collective-permute-start | bytes 786440 | tf_op jit(solution)/shard_map/ppermute | solution.py:149
  121.1 6.4 %collective-permute-start.16 = (bf16[256,512]{1,0:T(8,128)(2,1)}, bf16[256,512]{1,0:T(8,128)(2,1)S(1)}, u32[]{:S(2)}, u32[]{:S(2)}) collective-permute-start(bf16[256,512]{1,0:T(8,128)(2,1)} %get-tuple-element.14), channel_id=1, source_target_pairs={{0,1},{1,0},{2,3},{3,2},{4,5},{5,4},{6,7},{7,6},{8,9},{9,8},{10,11... | collective-permute-start | bytes 786440 | tf_op jit(solution)/shard_map/ppermute | solution.py:149
  (15 other events, 28.9 us)
where the time goes:
time: 131 us
  waiting for transfers between devices  53.8 us (41%)
  starting transfers between devices  31.5 us (24%)
  Pallas kernels  28.4 us (22%)
  local copies, waits for them, and re-layouts  9.49 us (7%)
  other arithmetic  7.35 us (6%)
    ppermute x10, waiting for transfers between devices, shift(): lax.ppermute(x, 'blk', [(i, (i + 2 * by) % blocks) for i in range(blocks)])  53.8 us
    ppermute x10, starting transfers between devices, shift(): lax.ppermute(x, 'blk', [(i, (i + 2 * by) % blocks) for i in range(blocks)])  21.7 us
    pallas_call x4, Pallas kernels, project(): pl.pallas_call(project_kernel, out_shape=(shape, shape), cost_estimate=pl...  16.6 us
    ppermute x6, starting transfers between devices, side(): return lax.ppermute(x, 'seq', [(i, i ^ bit) for i in range(seqs)])  8.08 us
    pallas_call x2, Pallas kernels, place(): pl.pallas_call(functools.partial(place_kernel, count), grid_spec=pltpu.Pr...  6.25 us
    pallas_call x1, Pallas kernels, attend(): pl.pallas_call(functools.partial(attend_kernel, heads, latents, tuple(pac...  5.48 us
    unnamed x42, local copies, waits for them, and re-layouts  5.27 us
    concatenate x2, other arithmetic, per_device(): both = jnp.concatenate([hidden, swap(hidden)], axis=0)  4.46 us
  transfers between devices with their start and end apart: 26, of which 10 were waited for; matrix products, arithmetic and copies ran while one was open for 8% of the time, Pallas kernels for 20%

commit v1 on v0

--- a/solution.py
+++ b/solution.py
@@ -102,19 +102,25 @@
 
 def steps(chips):
     far = chips // 2
-    order = [("kv_up", 1), ("kv_down", 1), ("a_up", 1), ("b_down", 1), ("kv_swap", 0)]
+    order = [("kv_up", 1), ("kv_down", 1)]
+    if far > 1:
+        order += [("w_up", 1), ("w_down", 1)]
+    order += [("kv_swap", 0)]
     for k in range(2, far + 1):
-        order += [("kv_up", k), ("kv_down", k), ("a_down", k - 1), ("b_up", k - 1)]
-        order += [("kv_swap_up", k - 1), ("kv_swap_down", k - 1), ("x_up", k - 1), ("y_down", k - 1)]
-        order += [("a_up", k), ("b_down", k)]
+        order += [("kv_up", k), ("kv_down", k), ("kv_swap_up", k - 1), ("kv_swap_down", k - 1)]
+        order += [("w_up" if k < far else "a_up", k), ("x_up", k - 1), ("y_up", k - 1)]
+        order += [("w_down" if k < far else "b_down", k), ("x_down", k - 1), ("y_down", k - 1)]
         if k > 2:
-            order += [("x_down", k - 2), ("y_up", k - 2)]
+            order += [("xy_up", k - 2), ("yx_up", k - 2), ("xy_down", k - 2), ("yx_down", k - 2)]
+    if far == 1:
+        order += [("a_up", far), ("b_down", far)]
     order += [("kv_swap_up", far), ("kv_swap_down", far), ("attend", 0), ("hidden_swap", 0)]
     if far > 1:
-        order += [("x_down", far - 1), ("y_up", far - 1)]
-    order += [("project", 0), ("x_up", far), ("y_down", far)]
+        order += [("xy_up", far - 1), ("yx_up", far - 1), ("xy_down", far - 1), ("yx_down", far - 1)]
+    order += [("project", 0), ("xa", far), ("ya", far), ("yb", far), ("xb", far)]
     for k in range(1, far):
         order += [("project_up", k), ("project_down", k)]
+    order += [("xya", far), ("yxb", far)]
     return order + [("place", 0), ("project", far), ("place", 1)]
 
 
@@ -124,23 +130,16 @@
     far = chips // 2
     me, seq = lax.axis_index("blk"), lax.axis_index("seq")
     chip, core = me // 2, me % 2
-    parity = (seq ^ (seq >> 1)) & 1
+    part = seq & 3
     heads = head_gate.shape[0]
     tokens, width = queries.shape[1:]
     latents = keys.shape[1]
 
-    half = out_weight.shape[0] // 2
-    quarter = half // 2
-    cols = out_weight.shape[1]
+    quarter = out_weight.shape[0] // 4
+    eighth = quarter // 2
     kv = jnp.concatenate([keys[0], values[0]], axis=0)
-    a = lax.dynamic_slice(out_weight, (parity * half, 0), (quarter, cols))
-    b = lax.dynamic_slice(out_weight, (parity * half + quarter, 0), (quarter, cols))
-
-    moved = {("kv_up", 0): kv, ("kv_down", 0): kv}
-    for name in ("a_up", "a_down"):
-        moved[name, 0] = a
-    for name in ("b_up", "b_down"):
-        moved[name, 0] = b
+    w = lax.dynamic_slice(out_weight, (part * quarter, 0), (quarter, out_weight.shape[1]))
+    moved = {("kv_up", 0): kv, ("kv_down", 0): kv, ("w_up", 0): w, ("w_down", 0): w}
 
     def shift(x, by):
         return lax.ppermute(x, "blk", [(i, (i + 2 * by) % blocks) for i in range(blocks)])
@@ -175,9 +174,12 @@
         )(jnp.tanh(head_gate)[None], image_index[0][:, None], latent_image, queries[0], *arrays)
 
     def units(k, name):
-        first = moved["a_up" if name != "down" else "a_down", k]
-        second = moved["b_down" if name != "up" else "b_up", k]
-        return [first, second, moved["x_down" if name == "down" else "x_up", k], moved["y_up" if name == "up" else "y_down", k]]
+        names = ["w_up", "x_up", "y_up", "xy_up", "yx_up"]
+        if name == "down":
+            names = ["w_down", "x_down", "y_down", "xy_down", "yx_down"]
+        elif name != "up":
+            names = ["a_up", "b_down", "xa", "xb", "ya", "yb", "xya", "yxb"]
+        return [moved[n, k] for n in names]
 
     mine, theirs, at = [], [], []
     out = None
@@ -186,23 +188,40 @@
         if name in ("kv_up", "kv_down") and k == far:
             before = moved[name, k - 1]
             moved[name, k] = shift(before[:latents] if name == "kv_up" else before[latents:], 1 if name == "kv_up" else -1)
-        elif name in ("kv_up", "a_up", "b_up"):
+        elif name == "a_up":
+            moved[name, k] = shift(moved["w_up", k - 1][:eighth], 1)
+        elif name == "b_down":
+            moved[name, k] = shift(moved["w_down", k - 1][eighth:], -1)
+        elif name in ("kv_up", "w_up"):
             moved[name, k] = shift(moved[name, k - 1], 1)
-        elif name in ("kv_down", "a_down", "b_down"):
+        elif name in ("kv_down", "w_down"):
             moved[name, k] = shift(moved[name, k - 1], -1)
         elif name == "kv_swap":
             moved[name, k] = swap(kv)
         elif name in ("kv_swap_up", "kv_swap_down"):
             moved[name, k] = swap(moved[name.replace("swap_", ""), k])
         elif name in ("x_up", "x_down"):
-            moved[name, k] = side(moved[name.replace("x", "a"), k], 1)
+            moved[name, k] = side(moved[name.replace("x", "w"), k], 1)
         elif name in ("y_up", "y_down"):
-            moved[name, k] = side(moved[name.replace("y", "b"), k], 2)
+            moved[name, k] = side(moved[name.replace("y", "w"), k], 2)
+        elif name in ("xy_up", "xy_down"):
+            moved[name, k] = side(moved[name.replace("xy", "x"), k][:eighth], 2)
+        elif name in ("yx_up", "yx_down"):
+            moved[name, k] = side(moved[name.replace("yx", "y"), k][eighth:], 1)
+        elif name in ("xa", "ya", "xb", "yb"):
+            moved[name, k] = side(moved["a_up" if "a" in name else "b_down", k], 1 if "x" in name else 2)
+        elif name == "xya":
+            moved[name, k] = side(moved["xa", k], 2)
+        elif name == "yxb":
+            moved[name, k] = side(moved["yb", k], 1)
         elif name == "attend":
             hidden = attend()
         elif name == "hidden_swap":
             both = jnp.concatenate([hidden, swap(hidden)], axis=0)
-            rolled = jnp.where(parity == 0, both, jnp.concatenate([both[:, half:], both[:, :half]], axis=1))
+            quarters = [
+                lax.dynamic_slice(both, (0, (part ^ r) * quarter), (2 * tokens, quarter)) for r in range(4)
+            ]
+            rolled = jnp.concatenate(quarters, axis=1)
         elif name == "place":
             out = place(core, at, mine, theirs, chips, out)
             mine, theirs, at = [], [], []

time: 131 us -> 121 us (0.924)
  waiting for transfers between devices: 53.8 us -> 36.2 us
  local copies, waits for them, and re-layouts: 9.49 us -> 14.6 us
  starting transfers between devices: 31.5 us -> 34.5 us
    ppermute x10 -> x8, waiting for transfers between devices: 53.8 us -> 29.8 us  [shift(): lax.ppermute(x, 'blk', [(i, (i + 2 * by) % blocks) for i in range(blocks)])]
    ppermute x6 -> x14, starting transfers between devices: 8.08 us -> 15.8 us  [side(): return lax.ppermute(x, 'seq', [(i, i ^ bit) for i in range(seqs)])]
    ppermute x6 -> x14, waiting for transfers between devices: 0.02 us -> 6.42 us  [side(): return lax.ppermute(x, 'seq', [(i, i ^ bit) for i in range(seqs)])]
    slice x0 -> x6, local copies, waits for them, and re-layouts: none -> 5.32 us  [the longest x2 2.64 us: per_device(): moved[name, k] = side(moved[name.replace('yx', 'y'), k][eighth:], 1)]
    ppermute x10 -> x8, starting transfers between devices: 21.7 us -> 16.8 us  [shift(): lax.ppermute(x, 'blk', [(i, (i + 2 * by) % blocks) for i in range(blocks)])]
    concatenate x2, other arithmetic: 4.46 us -> 1.71 us  [per_device(): both = jnp.concatenate([hidden, swap(hidden)], axis=0)]
    concatenate x0 -> x1, other arithmetic: none -> 1.63 us  [per_device(): rolled = jnp.concatenate(quarters, axis=1)]
    unnamed x42 -> x60, local copies, waits for them, and re-layouts: 5.27 us -> 5.88 us
  transfers between devices with their start and end apart: 26 -> 32, of which waited for: 10 -> 10; matrix products, arithmetic and copies ran while one was open for 8% -> 12% of each run, Pallas kernels for 20% -> 22%
where the time goes in v1:
time: 121 us; the launch traced here: 120 us
  waiting for transfers between devices  36.2 us (30%)
  starting transfers between devices  34.5 us (29%)
  Pallas kernels  28.4 us (23%)
  local copies, waits for them, and re-layouts  14.6 us (12%)
  other arithmetic  6.23 us (5%)
    ppermute x8, waiting for transfers between devices, shift(): lax.ppermute(x, 'blk', [(i, (i + 2 * by) % blocks) for i in range(blocks)])  29.8 us
    ppermute x8, starting transfers between devices, shift(): lax.ppermute(x, 'blk', [(i, (i + 2 * by) % blocks) for i in range(blocks)])  16.8 us
    pallas_call x4, Pallas kernels, project(): pl.pallas_call(project_kernel, out_shape=(shape, shape), cost_estimate=pl...  16.7 us
    ppermute x14, starting transfers between devices, side(): return lax.ppermute(x, 'seq', [(i, i ^ bit) for i in range(seqs)])  15.8 us
    ppermute x14, waiting for transfers between devices, side(): return lax.ppermute(x, 'seq', [(i, i ^ bit) for i in range(seqs)])  6.42 us
    pallas_call x2, Pallas kernels, place(): pl.pallas_call(functools.partial(place_kernel, count), grid_spec=pltpu.Pr...  6.25 us
    unnamed x60, local copies, waits for them, and re-layouts  5.88 us
    pallas_call x1, Pallas kernels, attend(): pl.pallas_call(functools.partial(attend_kernel, heads, latents, tuple(pac...  5.48 us
  transfers between devices with their start and end apart: 32, of which 10 were waited for; matrix products, arithmetic and copies ran while one was open for 12% of the time, Pallas kernels for 22%

profile of v1, /device:TPU:0, one launch (start us, length us, event | category | flops | bytes accessed | tf_op | source)
XLA Modules:
  0.0 120.2 jit_solution(1738077230165828857)
XLA Ops:
  1.6 2.6 %collective-permute-start.1 = (bf16[64,2048]{1,0:T(8,128)(2,1)S(1)}, bf16[64,2048]{1,0:T(8,128)(2,1)S(1)}, u32[]{:S(2)}, u32[]{:S(2)}) collective-permute-start(bf16[64,2048]{1,0:T(8,128)(2,1)S(1)} %pad_maximum_fusion.2.refs_0_), channel_id=1, source_target_pairs={{0,2},{1,3},{2,4},{3,5},{4,6},{5,7},{6,0},{7,1},{8,10},{9,11},{10,... | collective-permute-start | bytes 786440 | tf_op jit(solution)/shard_map/ppermute | solution.py:145
  4.2 2.1 %collective-permute-start.3 = (bf16[64,2048]{1,0:T(8,128)(2,1)S(1)}, bf16[64,2048]{1,0:T(8,128)(2,1)S(1)}, u32[]{:S(2)}, u32[]{:S(2)}) collective-permute-start(bf16[64,2048]{1,0:T(8,128)(2,1)S(1)} %pad_maximum_fusion.2.refs_0_), channel_id=1, source_target_pairs={{0,6},{1,7},{2,0},{3,1},{4,2},{5,3},{6,4},{7,5},{8,14},{9,15},{10,... | collective-permute-start | bytes 786440 | tf_op jit(solution)/shard_map/ppermute | solution.py:145
  6.3 1.9 %constant_dynamic-slice_fusion = bf16[512,512]{1,0:T(8,128)(2,1)} fusion(bf16[2048,512]{1,0:T(8,128)(2,1)} %refs_0_.1, s32[]{:T(128)S(6)} %select_n.32), kind=kLoop, calls=%fused_computation.17 | loop fusion | bytes 1048580 | tf_op jit(solution)/shard_map/dynamic_slice | solution.py:141
  8.4 5.0 %collective-permute-done.1.refs_2_ = bf16[64,2048]{1,0:T(8,128)(2,1)S(1)} collective-permute-done((bf16[64,2048]{1,0:T(8,128)(2,1)S(1)}, bf16[64,2048]{1,0:T(8,128)(2,1)S(1)}, u32[]{:S(2)}, u32[]{:S(2)}) %collective-permute-start.1) | collective-permute-done | bytes 262176 | tf_op jit(solution)/shard_map/ppermute | solution.py:145
  13.5 4.3 %collective-permute-start.5 = (bf16[32,2048]{1,0:T(8,128)(2,1)S(1)}, bf16[32,2048]{1,0:T(8,128)(2,1)S(1)}, u32[]{:S(2)}, u32[]{:S(2)}) collective-permute-start(bf16[32,2048]{1,0:T(8,128)(2,1)S(1)} %slice.32), channel_id=1, source_target_pairs={{0,2},{1,3},{2,4},{3,5},{4,6},{5,7},{6,0},{7,1},{8,10},{9,11},{10,... | collective-permute-start | bytes 393224 | tf_op jit(solution)/shard_map/ppermute | solution.py:145
  18.2 3.0 %collective-permute-start.6 = (bf16[32,2048]{1,0:T(8,128)(2,1)S(1)}, bf16[32,2048]{1,0:T(8,128)(2,1)S(1)}, u32[]{:S(2)}, u32[]{:S(2)}) collective-permute-start(bf16[32,2048]{1,0:T(8,128)(2,1)S(1)} %slice.33), channel_id=1, source_target_pairs={{0,6},{1,7},{2,0},{3,1},{4,2},{5,3},{6,4},{7,5},{8,14},{9,15},{10,... | collective-permute-start | bytes 393224 | tf_op jit(solution)/shard_map/ppermute | solution.py:145
  23.1 10.0 %collective-permute-done.5.refs_6_ = bf16[32,2048]{1,0:T(8,128)(2,1)S(1)} collective-permute-done((bf16[32,2048]{1,0:T(8,128)(2,1)S(1)}, bf16[32,2048]{1,0:T(8,128)(2,1)S(1)}, u32[]{:S(2)}, u32[]{:S(2)}) %collective-permute-start.5) | collective-permute-done | bytes 131104 | tf_op jit(solution)/shard_map/ppermute | solution.py:145
  33.2 2.5 %collective-permute-done.6.refs_7_ = bf16[32,2048]{1,0:T(8,128)(2,1)S(1)} collective-permute-done((bf16[32,2048]{1,0:T(8,128)(2,1)S(1)}, bf16[32,2048]{1,0:T(8,128)(2,1)S(1)}, u32[]{:S(2)}, u32[]{:S(2)}) %collective-permute-start.6) | collective-permute-done | bytes 131104 | tf_op jit(solution)/shard_map/ppermute | solution.py:145
  36.2 2.2 %collective-permute-start.12 = (bf16[512,512]{1,0:T(8,128)(2,1)}, bf16[512,512]{1,0:T(8,128)(2,1)S(1)}, u32[]{:S(2)}, u32[]{:S(2)}) collective-permute-start(bf16[512,512]{1,0:T(8,128)(2,1)} %constant_dynamic-slice_fusion), channel_id=1, source_target_pairs={{0,6},{1,7},{2,0},{3,1},{4,2},{5,3},{6,4},{7,5},{8,14},{9,15},{10,... | collective-permute-start | bytes 1572872 | tf_op jit(solution)/shard_map/ppermute | solution.py:145
  39.2 5.5 %attend.1 = bf16[256,2048]{1,0:T(8,128)(2,1)} custom-call(f32[1,16]{1,0:T(1,128)} %tanh_bitcast_fusion.gate_ref, s32[256,1]{1,0:T(8,128)} %copy.8.images_ref, s32[1,256]{1,0:T(1,128)} %and_select_fusion.latent_image_ref, bf16[256,2048]{1,0:T(8,128)(2,1)} %bitcast.20, bf16[64,2048]{1,0:T(8,128)(2,1)} %copy-done.4, bf16[64,2048]{1,0:T(8,128)(2,1)} %copy-done.7, ...), custom_call_target="tpu_custom_call" | custom-call | tf_op jit(solution)/shard_map/attend/pallas_call | solution.py:169
  44.8 1.6 %collective-permute-start.21 = (bf16[512,512]{1,0:T(8,128)(2,1)S(1)}, bf16[512,512]{1,0:T(8,128)(2,1)S(1)}, u32[]{:S(2)}, u32[]{:S(2)}) collective-permute-start(bf16[512,512]{1,0:T(8,128)(2,1)S(1)} %collective-permute-done.10.refs_0_), channel_id=1, source_target_pairs={{0,8},{8,0},{16,24},{24,16},{1,9},{9,1},{17,25},{25,17},{2,10},{10... | collective-permute-start | bytes 1572872 | tf_op jit(solution)/shard_map/ppermute | solution.py:151
  46.4 1.6 %collective-permute-start.22 = (bf16[512,512]{1,0:T(8,128)(2,1)S(1)}, bf16[512,512]{1,0:T(8,128)(2,1)}, u32[]{:S(2)}, u32[]{:S(2)}) collective-permute-start(bf16[512,512]{1,0:T(8,128)(2,1)S(1)} %collective-permute-done.10.refs_0_), channel_id=1, source_target_pairs={{0,16},{8,24},{16,0},{24,8},{1,17},{9,25},{17,1},{25,9},{2,18},{10... | collective-permute-start | bytes 1572872 | tf_op jit(solution)/shard_map/ppermute | solution.py:151
  48.0 3.1 %collective-permute-done.12.refs_0_ = bf16[512,512]{1,0:T(8,128)(2,1)S(1)} collective-permute-done((bf16[512,512]{1,0:T(8,128)(2,1)}, bf16[512,512]{1,0:T(8,128)(2,1)S(1)}, u32[]{:S(2)}, u32[]{:S(2)}) %collective-permute-start.12) | collective-permute-done | bytes 524320 | tf_op jit(solution)/shard_map/ppermute | solution.py:145
  51.1 1.7 %collective-permute-start.25 = (bf16[512,512]{1,0:T(8,128)(2,1)S(1)}, bf16[512,512]{1,0:T(8,128)(2,1)}, u32[]{:S(2)}, u32[]{:S(2)}) collective-permute-start(bf16[512,512]{1,0:T(8,128)(2,1)S(1)} %collective-permute-done.12.refs_0_), channel_id=1, source_target_pairs={{0,8},{8,0},{16,24},{24,16},{1,9},{9,1},{17,25},{25,17},{2,10},{10... | collective-permute-start | bytes 1572872 | tf_op jit(solution)/shard_map/ppermute | solution.py:151
  52.8 3.7 %collective-permute-done.11.refs_0_ = bf16[256,512]{1,0:T(8,128)(2,1)S(1)} collective-permute-done((bf16[256,512]{1,0:T(8,128)(2,1)S(1)}, bf16[256,512]{1,0:T(8,128)(2,1)S(1)}, u32[]{:S(2)}, u32[]{:S(2)}) %collective-permute-start.11) | collective-permute-done | bytes 262176 | tf_op jit(solution)/shard_map/ppermute | solution.py:145
  56.5 1.5 %collective-permute-start.26 = (bf16[512,512]{1,0:T(8,128)(2,1)S(1)}, bf16[512,512]{1,0:T(8,128)(2,1)}, u32[]{:S(2)}, u32[]{:S(2)}) collective-permute-start(bf16[512,512]{1,0:T(8,128)(2,1)S(1)} %collective-permute-done.12.refs_0_), channel_id=1, source_target_pairs={{0,16},{8,24},{16,0},{24,8},{1,17},{9,25},{17,1},{25,9},{2,18},{10... | collective-permute-start | bytes 1572872 | tf_op jit(solution)/shard_map/ppermute | solution.py:151
  60.4 2.6 %collective-permute-start.13 = (bf16[256,512]{1,0:T(8,128)(2,1)}, bf16[256,512]{1,0:T(8,128)(2,1)}, u32[]{:S(2)}, u32[]{:S(2)}) collective-permute-start(bf16[256,512]{1,0:T(8,128)(2,1)} %slice.35), channel_id=1, source_target_pairs={{0,6},{1,7},{2,0},{3,1},{4,2},{5,3},{6,4},{7,5},{8,14},{9,15},{10,... | collective-permute-start | bytes 786440 | tf_op jit(solution)/shard_map/ppermute | solution.py:145
  64.0 4.9 %collective-permute-done.13.refs_1_ = bf16[256,512]{1,0:T(8,128)(2,1)} collective-permute-done((bf16[256,512]{1,0:T(8,128)(2,1)}, bf16[256,512]{1,0:T(8,128)(2,1)}, u32[]{:S(2)}, u32[]{:S(2)}) %collective-permute-start.13) | collective-permute-done | bytes 262176 | tf_op jit(solution)/shard_map/ppermute | solution.py:145
  68.9 1.5 %collective-permute-start.14 = (bf16[256,512]{1,0:T(8,128)(2,1)S(1)}, bf16[256,512]{1,0:T(8,128)(2,1)}, u32[]{:S(2)}, u32[]{:S(2)}) collective-permute-start(bf16[256,512]{1,0:T(8,128)(2,1)S(1)} %collective-permute-done.11.refs_0_), channel_id=1, source_target_pairs={{0,8},{8,0},{16,24},{24,16},{1,9},{9,1},{17,25},{25,17},{2,10},{10... | collective-permute-start | bytes 786440 | tf_op jit(solution)/shard_map/ppermute | solution.py:151
  72.1 1.4 %collective-permute-start.23 = (bf16[256,512]{1,0:T(8,128)(2,1)S(1)}, bf16[256,512]{1,0:T(8,128)(2,1)S(1)}, u32[]{:S(2)}, u32[]{:S(2)}) collective-permute-start(bf16[256,512]{1,0:T(8,128)(2,1)S(1)} %slice.36), channel_id=1, source_target_pairs={{0,16},{8,24},{16,0},{24,8},{1,17},{9,25},{17,1},{25,9},{2,18},{10... | collective-permute-start | bytes 786440 | tf_op jit(solution)/shard_map/ppermute | solution.py:151
  75.1 1.7 %slice.39 = bf16[256,512]{1,0:T(8,128)(2,1)} slice(bf16[512,512]{1,0:T(8,128)(2,1)} %collective-permute-done.26.refs_2_), slice={[256:512], [0:512]} | slice | bytes 524288 | tf_op jit(solution)/shard_map/slice | solution.py:210
  77.7 1.6 %pad_maximum_fusion.1.hidden_ref = bf16[512,2048]{1,0:T(8,128)(2,1)} fusion(bf16[512,512]{1,0:T(8,128)(2,1)S(1)} %get-tuple-element.24, bf16[512,512]{1,0:T(8,128)(2,1)S(1)} %get-tuple-element.23, bf16[512,512]{1,0:T(8,128)(2,1)S(1)} %get-tuple-element.22, bf16[512,512]{1,0:T(8,128)(2,1)S(1)} %get-tuple-element.21), kind=kLoop, calls=%fused_computation.9 | loop fusion | flops 8388608 | bytes 4194304 | tf_op jit(solution)/shard_map/concatenate | solution.py:224
  79.3 1.5 %collective-permute-start.28 = (bf16[256,512]{1,0:T(8,128)(2,1)}, bf16[256,512]{1,0:T(8,128)(2,1)S(1)}, u32[]{:S(2)}, u32[]{:S(2)}) collective-permute-start(bf16[256,512]{1,0:T(8,128)(2,1)} %slice.39), channel_id=1, source_target_pairs={{0,8},{8,0},{16,24},{24,16},{1,9},{9,1},{17,25},{25,17},{2,10},{10... | collective-permute-start | bytes 786440 | tf_op jit(solution)/shard_map/ppermute | solution.py:151
  80.8 1.5 %pad_maximum_fusion.hidden_ref = bf16[512,2048]{1,0:T(8,128)(2,1)} fusion(bf16[256,2048]{1,0:T(8,128)(2,1)S(1)} %collective-permute-done.9, bf16[256,2048]{1,0:T(8,128)(2,1)S(1)} %copy-done), kind=kLoop, calls=%fused_computation.4 | loop fusion | flops 4194304 | bytes 4194304 | tf_op jit(solution)/shard_map/concatenate | solution.py:220
  82.8 2.6 %collective-permute-done.23.refs_3_ = bf16[256,512]{1,0:T(8,128)(2,1)S(1)} collective-permute-done((bf16[256,512]{1,0:T(8,128)(2,1)S(1)}, bf16[256,512]{1,0:T(8,128)(2,1)S(1)}, u32[]{:S(2)}, u32[]{:S(2)}) %collective-permute-start.23) | collective-permute-done | bytes 262176 | tf_op jit(solution)/shard_map/ppermute | solution.py:151
  88.2 3.0 %collective-permute-done.27.refs_3_ = bf16[256,512]{1,0:T(8,128)(2,1)} collective-permute-done((bf16[256,512]{1,0:T(8,128)(2,1)S(1)}, bf16[256,512]{1,0:T(8,128)(2,1)}, u32[]{:S(2)}, u32[]{:S(2)}) %collective-permute-start.27) | collective-permute-done | bytes 262176 | tf_op jit(solution)/shard_map/ppermute | solution.py:151
  91.7 4.3 %project.5 = (bf16[256,512]{1,0:T(8,128)(2,1)}, bf16[256,512]{1,0:T(8,128)(2,1)}) custom-call(bf16[512,2048]{1,0:T(8,128)(2,1)} %pad_maximum_fusion.hidden_ref, bf16[2048,512]{1,0:T(8,128)(2,1)} %refs_0_.1), custom_call_target="tpu_custom_call" | custom-call | flops 1073741824 | bytes 2097152 | tf_op jit(solution)/shard_map/project/pallas_call | solution.py:58
  95.9 4.2 %project.6 = (bf16[256,512]{1,0:T(8,128)(2,1)}, bf16[256,512]{1,0:T(8,128)(2,1)}) custom-call(bf16[512,2048]{1,0:T(8,128)(2,1)} %pad_maximum_fusion.1.hidden_ref, bf16[512,512]{1,0:T(8,128)(2,1)} %copy-done.1, bf16[512,512]{1,0:T(8,128)(2,1)} %copy-done.3, bf16[512,512]{1,0:T(8,128)(2,1)} %collective-permute-done.22.refs_2_, bf16[256,512]{1,0:T(8,128)(2,1)} %copy-done.9, ...), custom_call_target="tpu_custom_call" | custom-call | flops 1073741824 | bytes 2097152 | tf_op jit(solution)/shard_map/project/pallas_call | solution.py:58
  100.8 4.1 %project.7 = (bf16[256,512]{1,0:T(8,128)(2,1)}, bf16[256,512]{1,0:T(8,128)(2,1)}) custom-call(bf16[512,2048]{1,0:T(8,128)(2,1)} %pad_maximum_fusion.1.hidden_ref, bf16[512,512]{1,0:T(8,128)(2,1)} %copy-done.2, bf16[512,512]{1,0:T(8,128)(2,1)} %collective-permute-done.25.refs_1_, bf16[512,512]{1,0:T(8,128)(2,1)} %collective-permute-done.26.refs_2_, ...), custom_call_target="tpu_custom_call" | custom-call | flops 1073741824 | bytes 2097152 | tf_op jit(solution)/shard_map/project/pallas_call | solution.py:58
  106.9 4.1 %project.4 = (bf16[256,512]{1,0:T(8,128)(2,1)}, bf16[256,512]{1,0:T(8,128)(2,1)}) custom-call(bf16[512,2048]{1,0:T(8,128)(2,1)} %pad_maximum_fusion.1.hidden_ref, bf16[256,512]{1,0:T(8,128)(2,1)} %copy-done.8, bf16[256,512]{1,0:T(8,128)(2,1)} %collective-permute-done.13.refs_1_, bf16[256,512]{1,0:T(8,128)(2,1)} %collective-permute-done.14.refs_2_, ...), custom_call_target="tpu_custom_call" | custom-call | flops 1073741824 | bytes 2097152 | tf_op jit(solution)/shard_map/project/pallas_call | solution.py:58
  113.3 3.7 %place.2.refs_2_ = bf16[256,4096]{1,0:T(8,128)(2,1)} custom-call(s32[4]{0:T(128)} %pad_add_fusion.1.where_ref, bf16[256,512]{1,0:T(8,128)(2,1)} %get-tuple-element.15.refs_0_, bf16[256,512]{1,0:T(8,128)(2,1)} %get-tuple-element.16.refs_1_, bf16[256,512]{1,0:T(8,128)(2,1)} %get-tuple-element.17.refs_2_, bf16[256,512]{1,0:T(8,128)(2,1)} %copy-done.19, ...), custom_call_target="tpu_custom_call" | custom-call | tf_op jit(solution)/shard_map/place/pallas_call | solution.py:89
  117.7 2.5 %place.3 = bf16[256,4096]{1,0:T(8,128)(2,1)} custom-call(s32[2]{0:T(128)} %pad_add_fusion.where_ref, bf16[256,512]{1,0:T(8,128)(2,1)} %get-tuple-element.13.refs_0_, bf16[256,512]{1,0:T(8,128)(2,1)} %copy-done.18, bf16[256,4096]{1,0:T(8,128)(2,1)} %place.2.refs_2_), custom_call_target="tpu_custom_call", output_to_operand_aliasing={{}: (3, {})} | custom-call | tf_op jit(solution)/shard_map/place/pallas_call | solution.py:89
  (120 shorter events, 22.4 us)
Async XLA Ops:
  1.0 20.2 %collective-permute-start = (bf16[64,2048]{1,0:T(8,128)(2,1)S(1)}, bf16[64,2048]{1,0:T(8,128)(2,1)S(1)}, u32[]{:S(2)}, u32[]{:S(2)}) collective-permute-start(bf16[64,2048]{1,0:T(8,128)(2,1)S(1)} %pad_maximum_fusion.2.refs_0_), channel_id=1, source_target_pairs={{0,1},{1,0},{2,3},{3,2},{4,5},{5,4},{6,7},{7,6},{8,9},{9,8},{10,11... | collective-permute-start | bytes 786440 | tf_op jit(solution)/shard_map/ppermute | solution.py:148
  1.6 11.9 %collective-permute-start.1 = (bf16[64,2048]{1,0:T(8,128)(2,1)S(1)}, bf16[64,2048]{1,0:T(8,128)(2,1)S(1)}, u32[]{:S(2)}, u32[]{:S(2)}) collective-permute-start(bf16[64,2048]{1,0:T(8,128)(2,1)S(1)} %pad_maximum_fusion.2.refs_0_), channel_id=1, source_target_pairs={{0,2},{1,3},{2,4},{3,5},{4,6},{5,7},{6,0},{7,1},{8,10},{9,11},{10,... | collective-permute-start | bytes 786440 | tf_op jit(solution)/shard_map/ppermute | solution.py:145
  4.2 14.0 %collective-permute-start.3 = (bf16[64,2048]{1,0:T(8,128)(2,1)S(1)}, bf16[64,2048]{1,0:T(8,128)(2,1)S(1)}, u32[]{:S(2)}, u32[]{:S(2)}) collective-permute-start(bf16[64,2048]{1,0:T(8,128)(2,1)S(1)} %pad_maximum_fusion.2.refs_0_), channel_id=1, source_target_pairs={{0,6},{1,7},{2,0},{3,1},{4,2},{5,3},{6,4},{7,5},{8,14},{9,15},{10,... | collective-permute-start | bytes 786440 | tf_op jit(solution)/shard_map/ppermute | solution.py:145
  8.2 36.6 %collective-permute-start.10 = (bf16[512,512]{1,0:T(8,128)(2,1)}, bf16[512,512]{1,0:T(8,128)(2,1)S(1)}, u32[]{:S(2)}, u32[]{:S(2)}) collective-permute-start(bf16[512,512]{1,0:T(8,128)(2,1)} %constant_dynamic-slice_fusion), channel_id=1, source_target_pairs={{0,2},{1,3},{2,4},{3,5},{4,6},{5,7},{6,0},{7,1},{8,10},{9,11},{10,... | collective-permute-start | bytes 1572872 | tf_op jit(solution)/shard_map/ppermute | solution.py:145
  13.5 19.7 %collective-permute-start.5 = (bf16[32,2048]{1,0:T(8,128)(2,1)S(1)}, bf16[32,2048]{1,0:T(8,128)(2,1)S(1)}, u32[]{:S(2)}, u32[]{:S(2)}) collective-permute-start(bf16[32,2048]{1,0:T(8,128)(2,1)S(1)} %slice.32), channel_id=1, source_target_pairs={{0,2},{1,3},{2,4},{3,5},{4,6},{5,7},{6,0},{7,1},{8,10},{9,11},{10,... | collective-permute-start | bytes 393224 | tf_op jit(solution)/shard_map/ppermute | solution.py:145
  18.2 17.4 %collective-permute-start.6 = (bf16[32,2048]{1,0:T(8,128)(2,1)S(1)}, bf16[32,2048]{1,0:T(8,128)(2,1)S(1)}, u32[]{:S(2)}, u32[]{:S(2)}) collective-permute-start(bf16[32,2048]{1,0:T(8,128)(2,1)S(1)} %slice.33), channel_id=1, source_target_pairs={{0,6},{1,7},{2,0},{3,1},{4,2},{5,3},{6,4},{7,5},{8,14},{9,15},{10,... | collective-permute-start | bytes 393224 | tf_op jit(solution)/shard_map/ppermute | solution.py:145
  21.2 15.0 %collective-permute-start.2 = (bf16[64,2048]{1,0:T(8,128)(2,1)S(1)}, bf16[64,2048]{1,0:T(8,128)(2,1)S(1)}, u32[]{:S(2)}, u32[]{:S(2)}) collective-permute-start(bf16[64,2048]{1,0:T(8,128)(2,1)S(1)} %collective-permute-done.1.refs_2_), channel_id=1, source_target_pairs={{0,1},{1,0},{2,3},{3,2},{4,5},{5,4},{6,7},{7,6},{8,9},{9,8},{10,11... | collective-permute-start | bytes 786440 | tf_op jit(solution)/shard_map/ppermute | solution.py:148
  21.2 17.2 %collective-permute-start.4 = (bf16[64,2048]{1,0:T(8,128)(2,1)S(1)}, bf16[64,2048]{1,0:T(8,128)(2,1)S(1)}, u32[]{:S(2)}, u32[]{:S(2)}) collective-permute-start(bf16[64,2048]{1,0:T(8,128)(2,1)S(1)} %collective-permute-done.3.refs_4_), channel_id=1, source_target_pairs={{0,1},{1,0},{2,3},{3,2},{4,5},{5,4},{6,7},{7,6},{8,9},{9,8},{10,11... | collective-permute-start | bytes 786440 | tf_op jit(solution)/shard_map/ppermute | solution.py:148
  33.1 5.3 %collective-permute-start.7 = (bf16[32,2048]{1,0:T(8,128)(2,1)S(1)}, bf16[32,2048]{1,0:T(8,128)(2,1)S(1)}, u32[]{:S(2)}, u32[]{:S(2)}) collective-permute-start(bf16[32,2048]{1,0:T(8,128)(2,1)S(1)} %collective-permute-done.5.refs_6_), channel_id=1, source_target_pairs={{0,1},{1,0},{2,3},{3,2},{4,5},{5,4},{6,7},{7,6},{8,9},{9,8},{10,11... | collective-permute-start | bytes 393224 | tf_op jit(solution)/shard_map/ppermute | solution.py:148
  35.7 2.8 %collective-permute-start.8 = (bf16[32,2048]{1,0:T(8,128)(2,1)S(1)}, bf16[32,2048]{1,0:T(8,128)(2,1)S(1)}, u32[]{:S(2)}, u32[]{:S(2)}) collective-permute-start(bf16[32,2048]{1,0:T(8,128)(2,1)S(1)} %collective-permute-done.6.refs_7_), channel_id=1, source_target_pairs={{0,1},{1,0},{2,3},{3,2},{4,5},{5,4},{6,7},{7,6},{8,9},{9,8},{10,11... | collective-permute-start | bytes 393224 | tf_op jit(solution)/shard_map/ppermute | solution.py:148
  36.2 14.9 %collective-permute-start.12 = (bf16[512,512]{1,0:T(8,128)(2,1)}, bf16[512,512]{1,0:T(8,128)(2,1)S(1)}, u32[]{:S(2)}, u32[]{:S(2)}) collective-permute-start(bf16[512,512]{1,0:T(8,128)(2,1)} %constant_dynamic-slice_fusion), channel_id=1, source_target_pairs={{0,6},{1,7},{2,0},{3,1},{4,2},{5,3},{6,4},{7,5},{8,14},{9,15},{10,... | collective-permute-start | bytes 1572872 | tf_op jit(solution)/shard_map/ppermute | solution.py:145
  44.7 32.0 %collective-permute-start.9 = (bf16[256,2048]{1,0:T(8,128)(2,1)}, bf16[256,2048]{1,0:T(8,128)(2,1)S(1)}, u32[]{:S(2)}, u32[]{:S(2)}) collective-permute-start(bf16[256,2048]{1,0:T(8,128)(2,1)} %attend.1), channel_id=1, source_target_pairs={{0,1},{1,0},{2,3},{3,2},{4,5},{5,4},{6,7},{7,6},{8,9},{9,8},{10,11... | collective-permute-start | bytes 3145736 | tf_op jit(solution)/shard_map/ppermute | solution.py:148
  44.8 14.9 %collective-permute-start.21 = (bf16[512,512]{1,0:T(8,128)(2,1)S(1)}, bf16[512,512]{1,0:T(8,128)(2,1)S(1)}, u32[]{:S(2)}, u32[]{:S(2)}) collective-permute-start(bf16[512,512]{1,0:T(8,128)(2,1)S(1)} %collective-permute-done.10.refs_0_), channel_id=1, source_target_pairs={{0,8},{8,0},{16,24},{24,16},{1,9},{9,1},{17,25},{25,17},{2,10},{10... | collective-permute-start | bytes 1572872 | tf_op jit(solution)/shard_map/ppermute | solution.py:151
  46.3 10.2 %collective-permute-start.11 = (bf16[256,512]{1,0:T(8,128)(2,1)S(1)}, bf16[256,512]{1,0:T(8,128)(2,1)S(1)}, u32[]{:S(2)}, u32[]{:S(2)}) collective-permute-start(bf16[256,512]{1,0:T(8,128)(2,1)S(1)} %slice.34), channel_id=1, source_target_pairs={{0,2},{1,3},{2,4},{3,5},{4,6},{5,7},{6,0},{7,1},{8,10},{9,11},{10,... | collective-permute-start | bytes 786440 | tf_op jit(solution)/shard_map/ppermute | solution.py:145
  46.4 24.0 %collective-permute-start.22 = (bf16[512,512]{1,0:T(8,128)(2,1)S(1)}, bf16[512,512]{1,0:T(8,128)(2,1)}, u32[]{:S(2)}, u32[]{:S(2)}) collective-permute-start(bf16[512,512]{1,0:T(8,128)(2,1)S(1)} %collective-permute-done.10.refs_0_), channel_id=1, source_target_pairs={{0,16},{8,24},{16,0},{24,8},{1,17},{9,25},{17,1},{25,9},{2,18},{10... | collective-permute-start | bytes 1572872 | tf_op jit(solution)/shard_map/ppermute | solution.py:151
  51.1 20.9 %collective-permute-start.25 = (bf16[512,512]{1,0:T(8,128)(2,1)S(1)}, bf16[512,512]{1,0:T(8,128)(2,1)}, u32[]{:S(2)}, u32[]{:S(2)}) collective-permute-start(bf16[512,512]{1,0:T(8,128)(2,1)S(1)} %collective-permute-done.12.refs_0_), channel_id=1, source_target_pairs={{0,8},{8,0},{16,24},{24,16},{1,9},{9,1},{17,25},{25,17},{2,10},{10... | collective-permute-start | bytes 1572872 | tf_op jit(solution)/shard_map/ppermute | solution.py:151
  56.5 17.9 %collective-permute-start.26 = (bf16[512,512]{1,0:T(8,128)(2,1)S(1)}, bf16[512,512]{1,0:T(8,128)(2,1)}, u32[]{:S(2)}, u32[]{:S(2)}) collective-permute-start(bf16[512,512]{1,0:T(8,128)(2,1)S(1)} %collective-permute-done.12.refs_0_), channel_id=1, source_target_pairs={{0,16},{8,24},{16,0},{24,8},{1,17},{9,25},{17,1},{25,9},{2,18},{10... | collective-permute-start | bytes 1572872 | tf_op jit(solution)/shard_map/ppermute | solution.py:151
  60.4 8.5 %collective-permute-start.13 = (bf16[256,512]{1,0:T(8,128)(2,1)}, bf16[256,512]{1,0:T(8,128)(2,1)}, u32[]{:S(2)}, u32[]{:S(2)}) collective-permute-start(bf16[256,512]{1,0:T(8,128)(2,1)} %slice.35), channel_id=1, source_target_pairs={{0,6},{1,7},{2,0},{3,1},{4,2},{5,3},{6,4},{7,5},{8,14},{9,15},{10,... | collective-permute-start | bytes 786440 | tf_op jit(solution)/shard_map/ppermute | solution.py:145
  68.9 10.4 %collective-permute-start.14 = (bf16[256,512]{1,0:T(8,128)(2,1)S(1)}, bf16[256,512]{1,0:T(8,128)(2,1)}, u32[]{:S(2)}, u32[]{:S(2)}) collective-permute-start(bf16[256,512]{1,0:T(8,128)(2,1)S(1)} %collective-permute-done.11.refs_0_), channel_id=1, source_target_pairs={{0,8},{8,0},{16,24},{24,16},{1,9},{9,1},{17,25},{25,17},{2,10},{10... | collective-permute-start | bytes 786440 | tf_op jit(solution)/shard_map/ppermute | solution.py:151
  70.4 11.9 %collective-permute-start.17 = (bf16[256,512]{1,0:T(8,128)(2,1)}, bf16[256,512]{1,0:T(8,128)(2,1)}, u32[]{:S(2)}, u32[]{:S(2)}) collective-permute-start(bf16[256,512]{1,0:T(8,128)(2,1)} %collective-permute-done.13.refs_1_), channel_id=1, source_target_pairs={{0,16},{8,24},{16,0},{24,8},{1,17},{9,25},{17,1},{25,9},{2,18},{10... | collective-permute-start | bytes 786440 | tf_op jit(solution)/shard_map/ppermute | solution.py:151
  72.1 13.3 %collective-permute-start.23 = (bf16[256,512]{1,0:T(8,128)(2,1)S(1)}, bf16[256,512]{1,0:T(8,128)(2,1)S(1)}, u32[]{:S(2)}, u32[]{:S(2)}) collective-permute-start(bf16[256,512]{1,0:T(8,128)(2,1)S(1)} %slice.36), channel_id=1, source_target_pairs={{0,16},{8,24},{16,0},{24,8},{1,17},{9,25},{17,1},{25,9},{2,18},{10... | collective-permute-start | bytes 786440 | tf_op jit(solution)/shard_map/ppermute | solution.py:151
  74.5 11.7 %collective-permute-start.24 = (bf16[256,512]{1,0:T(8,128)(2,1)S(1)}, bf16[256,512]{1,0:T(8,128)(2,1)S(1)}, u32[]{:S(2)}, u32[]{:S(2)}) collective-permute-start(bf16[256,512]{1,0:T(8,128)(2,1)S(1)} %slice.37), channel_id=1, source_target_pairs={{0,8},{8,0},{16,24},{24,16},{1,9},{9,1},{17,25},{25,17},{2,10},{10... | collective-permute-start | bytes 786440 | tf_op jit(solution)/shard_map/ppermute | solution.py:151
  76.7 14.4 %collective-permute-start.27 = (bf16[256,512]{1,0:T(8,128)(2,1)S(1)}, bf16[256,512]{1,0:T(8,128)(2,1)}, u32[]{:S(2)}, u32[]{:S(2)}) collective-permute-start(bf16[256,512]{1,0:T(8,128)(2,1)S(1)} %slice.38), channel_id=1, source_target_pairs={{0,16},{8,24},{16,0},{24,8},{1,17},{9,25},{17,1},{25,9},{2,18},{10... | collective-permute-start | bytes 786440 | tf_op jit(solution)/shard_map/ppermute | solution.py:151
  79.3 20.8 %collective-permute-start.28 = (bf16[256,512]{1,0:T(8,128)(2,1)}, bf16[256,512]{1,0:T(8,128)(2,1)S(1)}, u32[]{:S(2)}, u32[]{:S(2)}) collective-permute-start(bf16[256,512]{1,0:T(8,128)(2,1)} %slice.39), channel_id=1, source_target_pairs={{0,8},{8,0},{16,24},{24,16},{1,9},{9,1},{17,25},{25,17},{2,10},{10... | collective-permute-start | bytes 786440 | tf_op jit(solution)/shard_map/ppermute | solution.py:151
  82.3 22.6 %collective-permute-start.15 = (bf16[256,512]{1,0:T(8,128)(2,1)}, bf16[256,512]{1,0:T(8,128)(2,1)S(1)}, u32[]{:S(2)}, u32[]{:S(2)}) collective-permute-start(bf16[256,512]{1,0:T(8,128)(2,1)} %collective-permute-done.13.refs_1_), channel_id=1, source_target_pairs={{0,8},{8,0},{16,24},{24,16},{1,9},{9,1},{17,25},{25,17},{2,10},{10... | collective-permute-start | bytes 786440 | tf_op jit(solution)/shard_map/ppermute | solution.py:151
  85.4 19.6 %collective-permute-start.16 = (bf16[256,512]{1,0:T(8,128)(2,1)S(1)}, bf16[256,512]{1,0:T(8,128)(2,1)S(1)}, u32[]{:S(2)}, u32[]{:S(2)}) collective-permute-start(bf16[256,512]{1,0:T(8,128)(2,1)S(1)} %collective-permute-done.11.refs_0_), channel_id=1, source_target_pairs={{0,16},{8,24},{16,0},{24,8},{1,17},{9,25},{17,1},{25,9},{2,18},{10... | collective-permute-start | bytes 786440 | tf_op jit(solution)/shard_map/ppermute | solution.py:151
  86.9 18.7 %collective-permute-start.18 = (bf16[256,512]{1,0:T(8,128)(2,1)}, bf16[256,512]{1,0:T(8,128)(2,1)S(1)}, u32[]{:S(2)}, u32[]{:S(2)}) collective-permute-start(bf16[256,512]{1,0:T(8,128)(2,1)} %collective-permute-done.14.refs_2_), channel_id=1, source_target_pairs={{0,16},{8,24},{16,0},{24,8},{1,17},{9,25},{17,1},{25,9},{2,18},{10... | collective-permute-start | bytes 786440 | tf_op jit(solution)/shard_map/ppermute | solution.py:151
  91.1 14.4 %collective-permute-start.19 = (bf16[256,512]{1,0:T(8,128)(2,1)}, bf16[256,512]{1,0:T(8,128)(2,1)S(1)}, u32[]{:S(2)}, u32[]{:S(2)}) collective-permute-start(bf16[256,512]{1,0:T(8,128)(2,1)} %collective-permute-done.17.refs_5_), channel_id=1, source_target_pairs={{0,8},{8,0},{16,24},{24,16},{1,9},{9,1},{17,25},{25,17},{2,10},{10... | collective-permute-start | bytes 786440 | tf_op jit(solution)/shard_map/ppermute | solution.py:151
  100.1 12.3 %collective-permute-start.29 = (bf16[256,512]{1,0:T(8,128)(2,1)S(1)}, bf16[256,512]{1,0:T(8,128)(2,1)S(1)}, u32[]{:S(2)}, u32[]{:S(2)}) collective-permute-start(bf16[256,512]{1,0:T(8,128)(2,1)S(1)} %copy-done.27), channel_id=1, source_target_pairs={{0,1},{1,0},{2,3},{3,2},{4,5},{5,4},{6,7},{7,6},{8,9},{9,8},{10,11... | collective-permute-start | bytes 786440 | tf_op jit(solution)/shard_map/ppermute | solution.py:148
  104.9 7.5 %collective-permute-start.30 = (bf16[256,512]{1,0:T(8,128)(2,1)S(1)}, bf16[256,512]{1,0:T(8,128)(2,1)S(1)}, u32[]{:S(2)}, u32[]{:S(2)}) collective-permute-start(bf16[256,512]{1,0:T(8,128)(2,1)S(1)} %copy-done.28), channel_id=1, source_target_pairs={{0,1},{1,0},{2,3},{3,2},{4,5},{5,4},{6,7},{7,6},{8,9},{9,8},{10,11... | collective-permute-start | bytes 786440 | tf_op jit(solution)/shard_map/ppermute | solution.py:148
  105.0 7.4 %collective-permute-start.31 = (bf16[256,512]{1,0:T(8,128)(2,1)}, bf16[256,512]{1,0:T(8,128)(2,1)S(1)}, u32[]{:S(2)}, u32[]{:S(2)}) collective-permute-start(bf16[256,512]{1,0:T(8,128)(2,1)} %get-tuple-element.20), channel_id=1, source_target_pairs={{0,1},{1,0},{2,3},{3,2},{4,5},{5,4},{6,7},{7,6},{8,9},{9,8},{10,11... | collective-permute-start | bytes 786440 | tf_op jit(solution)/shard_map/ppermute | solution.py:148
  111.1 5.9 %collective-permute-start.20 = (bf16[256,512]{1,0:T(8,128)(2,1)}, bf16[256,512]{1,0:T(8,128)(2,1)S(1)}, u32[]{:S(2)}, u32[]{:S(2)}) collective-permute-start(bf16[256,512]{1,0:T(8,128)(2,1)} %get-tuple-element.14), channel_id=1, source_target_pairs={{0,1},{1,0},{2,3},{3,2},{4,5},{5,4},{6,7},{7,6},{8,9},{9,8},{10,11... | collective-permute-start | bytes 786440 | tf_op jit(solution)/shard_map/ppermute | solution.py:148
  (30 other events, 309.7 us)
